TPU v7x, 128 devices: a whole 4x4x4 slice. The times are simulated.
128 devices in a mesh: dp: 16 (over y, x_hi, core), fsdp: 8 (over z, x_lo).
Axes of the slice: x: 4 (x_hi: 2, x_lo: 2; x = x_hi * 2 + x_lo), y: 4, z: 4, core: 2. Of those that a mesh axis runs over, the one named last changes fastest.
Arguments:
- acts: bfloat16 [65536, 8192], P(('dp', 'fsdp')), may hold values from -24 to 24
- grad_out: bfloat16 [65536, 1024], P(('dp', 'fsdp')), may hold values from -24 to 24
- codes: int32 [128, 16, 1024], P('fsdp'), may hold values from 0 to 65535
- scale_codes: int32 [128, 1024], P('fsdp'), may hold values from 0 to 255
- col_scale: float32 [1024], replicated, may hold values from 0.03 to 0.3
- down_adapter: bfloat16 [64, 8192], P(None, 'fsdp'), may hold values from -0.1796875 to 0.1796875
- up_adapter: bfloat16 [64, 1024], P(None, 'fsdp'), may hold values from -0.1875 to 0.1875
Outputs:
- input_gradient: bfloat16 [65536, 8192], P(('dp', 'fsdp'))
- grad_down: float32 [64, 8192], P(None, 'fsdp')
- grad_up: float32 [64, 1024], P(None, 'fsdp')
All inputs are finite; a program needn't handle non-finite values.
Results may differ from a plain program's by a relative error of at most 0.0059.
Values may be sent and summed in bfloat16 or wider, within the bound.
No kernel may reach another device: no remote copies, remote signals or barrier semaphores. Data moves between devices by JAX's collectives and lax.ppermute only.
A program may use at most 128 MiB of HBM per device.

v0:
```python
import jax
import jax.numpy as jnp
from jax import lax
from jax.sharding import PartitionSpec as P

adapter_scale = 0.5
nf4_table = [
    -1.0,
    -0.6961928009986877,
    -0.5250730514526367,
    -0.39491748809814453,
    -0.28444138169288635,
    -0.18477343022823334,
    -0.09105003625154495,
    0.0,
    0.07958029955625534,
    0.16093020141124725,
    0.24611230194568634,
    0.33791524171829224,
    0.44070982933044434,
    0.5626170039176941,
    0.7229568362236023,
    1.0,
]


def joined_along(tiles, dim):
    tiles = jnp.moveaxis(tiles, 0, dim)
    lengths = tiles.shape
    return tiles.reshape(*lengths[:dim], lengths[dim] * lengths[dim + 1], *lengths[dim + 2 :])


def gather_packed(arrays, axis, dims):
    flat = jnp.concatenate([a.reshape(-1) for a in arrays])
    lines, at, gathered = (lax.all_gather(flat, axis), 0, [])
    for a, dim in zip(arrays, dims):
        tiles = lines[:, at : at + a.size].reshape(-1, *a.shape)
        gathered.append(joined_along(tiles, dim))
        at += a.size
    return tuple(gathered)


def in_blocks(value, dim, length):
    before, after = (value.shape[:dim], value.shape[dim + 1 :])
    return jnp.moveaxis(value.reshape(*before, length, -1, *after), dim, 0)


def sum_at_owner(value, axis, dim):
    tiles = in_blocks(value, dim, lax.axis_size(axis))
    arrived = lax.all_to_all(tiles, axis, split_axis=0, concat_axis=0, tiled=True)
    return arrived.astype(jnp.float32).sum(axis=0)


def copy_for_each(value, axis):
    length = lax.axis_size(axis)
    return lax.all_to_all(
        jnp.broadcast_to(value[None], (length, *value.shape)), axis, 0, 0, tiled=True
    )


def taken_together(value, axis):
    everything = copy_for_each(value, axis)
    return jnp.sum(everything.astype(jnp.float32), axis=0)


def dequantize(codes, scale_codes, col_scale):
    block_count = codes.shape[0]
    columns = codes.shape[2]
    nibbles = jnp.stack([codes >> 4 * nibble_pos & 15 for nibble_pos in range(4)], axis=2)
    levels = jnp.zeros(nibbles.shape, jnp.float32)
    for position, quantum in enumerate(nf4_table):
        levels = jnp.where(nibbles == position, jnp.float32(quantum), levels)
    absmax = (scale_codes.astype(jnp.float32) + 1.0) / 256.0 * col_scale[None, :]
    weight = levels * absmax[:, None, None, :]
    return weight.reshape(block_count * 64, columns).astype(jnp.bfloat16)


def local(acts, grad_out, codes, scale_codes, col_scale, down_adapter, up_adapter):
    down_full, up_full = gather_packed((down_adapter, up_adapter), "fsdp", (1, 1))
    mixed = jnp.dot(grad_out, up_full.T, preferred_element_type=jnp.float32).astype(jnp.bfloat16)
    lowered = jnp.dot(acts, down_full.T, preferred_element_type=jnp.float32).astype(jnp.bfloat16)
    token_count = acts.shape[0] * lax.axis_size("dp") * lax.axis_size("fsdp")
    scale_factor = adapter_scale * float(token_count) ** (-0.5)
    local_rows = dequantize(codes, scale_codes, col_scale)
    frozen_base = lax.dot_general(
        grad_out,
        lax.all_gather(local_rows, "fsdp", axis=0, tiled=True),
        (((1,), (1,)), ((), ())),
        preferred_element_type=jnp.float32,
    )
    operand_side = jnp.dot(mixed, down_full, preferred_element_type=jnp.float32)
    input_gradient = (frozen_base + adapter_scale * operand_side).astype(jnp.bfloat16)
    term_down = lax.dot_general(
        mixed, acts, (((0,), (0,)), ((), ())), preferred_element_type=jnp.float32
    )
    term_up = lax.dot_general(
        lowered, grad_out, (((0,), (0,)), ((), ())), preferred_element_type=jnp.float32
    )
    shard_down = sum_at_owner(term_down.astype(jnp.bfloat16), "fsdp", 1)
    shard_up = sum_at_owner(term_up.astype(jnp.bfloat16), "fsdp", 1)
    summed_down = taken_together(shard_down.astype(jnp.bfloat16), "dp").astype(jnp.float32)
    summed_up = taken_together(shard_up.astype(jnp.bfloat16), "dp").astype(jnp.float32)
    grad_down = scale_factor * summed_down
    grad_up = scale_factor * summed_up
    return (input_gradient, grad_down, grad_up)


def solution(mesh):
    placed = (
        P(("dp", "fsdp"), None),
        P(("dp", "fsdp"), None),
        P("fsdp", None, None),
        P("fsdp", None),
        P(),
        P(None, "fsdp"),
        P(None, "fsdp"),
    )
    return jax.shard_map(
        local,
        mesh=mesh,
        in_specs=placed,
        out_specs=(P(("dp", "fsdp"), None), P(None, "fsdp"), P(None, "fsdp")),
        check_vma=False,
    )
```

profile of v0, /device:TPU:1, one launch (start us, length us, event | category | flops | bytes accessed | tf_op | source)
XLA Modules:
  0.0 462.1 jit_solution(7870341430328449806)
XLA Ops:
  7.2 0.0 copy-start
  7.2 0.0 all-gather.6.cloned.1.call-start
  7.2 1.0 copy.31
  8.2 1.4 pad_maximum_fusion
  9.6 0.0 all-gather.6.cloned.1.call-update
  9.6 0.0 all-gather.4.cloned.1.call-start
  9.7 1.5 and_bitcast_fusion.3
  11.2 0.0 copy-start.2
  11.2 0.0 copy-start.3
  11.2 0.9 copy-done.2
  12.2 0.4 copy-done.3
  12.5 4.1 select_select_fusion
  16.6 4.8 %copy.23 = f32[16,16,4,1024]{3,2,1,0:T(4,128)} copy(f32[16,16,4,1024]{3,1,0,2:T(8,128)S(1)} %select_select_fusion) | data formatting | bytes 8388608 | tf_op jit(solution)/shard_map/jit(_where)/select_n | solution.py:72
  21.5 5.3 %reshape.108 = f32[1024,1024]{1,0:T(8,128)} reshape(f32[16,16,4,1024]{3,2,1,0:T(4,128)} %copy.23) | data formatting | bytes 8388608 | tf_op jit(solution)/shard_map/jit(_where)/select_n | solution.py:72
  26.8 0.0 copy-start.5
  26.8 0.0 copy-start.4
  26.8 2.2 fusion.1
  29.0 2.1 copy.22
  31.1 0.7 eq.156
  31.8 0.0 copy-done.5
  31.8 0.0 copy-done.4
  31.8 3.1 mul.45
  34.9 5.3 %mul.46 = f32[1024,1024]{1,0:T(8,128)} reshape(f32[16,16,4,1024]{3,2,1,0:T(4,128)} %mul.45) | data formatting | bytes 8388608 | tf_op jit(solution)/shard_map/mul | solution.py:74
  40.2 6.0 %multiply_convert_fusion = bf16[1024,1024]{1,0:T(8,128)(2,1)} fusion(f32[1024,1024]{1,0:T(8,128)} %mul.46, pred[1024,1024]{1,0:T(8,128)(4,1)S(1)} %eq.156, f32[1024,1024]{1,0:T(8,128)} %reshape.108), kind=kLoop, calls=%fused_computation.6 | loop fusion | flops 3145728 | bytes 11534336 | tf_op jit(solution)/shard_map/convert_element_type | solution.py:75
  46.3 0.0 all-gather.4.cloned.1.call-update
  46.3 2.7 all-gather.6.cloned.1.call-done
  49.0 1.8 reshape.92
  50.7 0.1 slice.9
  50.8 0.6 copy.33
  51.4 0.0 copy-done
  51.4 6.3 %fusion.2 = bf16[8,8,8,128]{3,2,1,0:T(8,128)(2,1)S(1)} fusion(bf16[512,1024]{1,0:T(8,128)(2,1)S(1)} %copy-done, bf16[64,8192]{1,0:T(8,128)(2,1)S(1)} %bitcast.52, bf16[512,8192]{1,0:T(8,128)(2,1)} %param.7), kind=kOutput, calls=%fused_computation.9 | convolution fusion | flops 604078080 | bytes 10616832 | tf_op jit(solution)/shard_map/dot_general | solution.py:96
  57.7 0.7 copy.41
  58.4 4.1 all-to-all-start.2
  62.5 0.4 convolution_convert_fusion.2
  63.0 5.6 %convolution_convert_fusion = bf16[64,8192]{1,0:T(8,128)(2,1)S(1)} fusion(bf16[64,512]{1,0:T(8,128)(2,1)S(1)} %convolution_convert_fusion.2, bf16[512,8192]{1,0:T(8,128)(2,1)} %param.7), kind=kOutput, calls=%fused_computation.2 | convolution fusion | flops 537395200 | bytes 9502720 | tf_op jit(solution)/shard_map/dot_general | solution.py:93
  68.6 1.1 copy.40
  69.7 0.0 all-to-all-done.2
  69.7 5.1 %all-to-all-start = ((bf16[8,64,1024]{2,1,0:T(8,128)(2,1)}), bf16[8,64,1024]{2,1,0:T(8,128)(2,1)S(1)}, u32[]{:S(2)}, u32[]{:S(2)}) async-start(bf16[8,64,1024]{2,1,0:T(8,128)(2,1)} %bitcast.54), calls=%async_computation | async-start | bytes 2097152 | tf_op jit(solution)/shard_map/all_to_all | solution.py:50
  74.8 25.6 %all-to-all-done = bf16[8,64,1024]{2,1,0:T(8,128)(2,1)S(1)} async-done(((bf16[8,64,1024]{2,1,0:T(8,128)(2,1)}), bf16[8,64,1024]{2,1,0:T(8,128)(2,1)S(1)}, u32[]{:S(2)}, u32[]{:S(2)}) %all-to-all-start) | async-done | bytes 1048608 | tf_op jit(solution)/shard_map/all_to_all | solution.py:50
  100.3 0.8 broadcast_in_dim.84
  101.1 12.4 %all-to-all-start.3 = ((bf16[16,64,128]{2,1,0:T(8,128)(2,1)}), bf16[16,64,128]{2,1,0:T(8,128)(2,1)S(1)}, u32[]{:S(2)}, u32[]{:S(2)}) async-start(bf16[16,64,128]{2,1,0:T(8,128)(2,1)} %broadcast_in_dim.84), calls=%async_computation.3 | async-start | bytes 524288 | tf_op jit(solution)/shard_map/all_to_all | solution.py:56
  113.5 0.8 reduce_sum.42
  114.4 11.2 %all-to-all-done.3 = bf16[16,64,128]{2,1,0:T(8,128)(2,1)S(1)} async-done(((bf16[16,64,128]{2,1,0:T(8,128)(2,1)}), bf16[16,64,128]{2,1,0:T(8,128)(2,1)S(1)}, u32[]{:S(2)}, u32[]{:S(2)}) %all-to-all-start.3) | async-done | bytes 262176 | tf_op jit(solution)/shard_map/all_to_all | solution.py:56
  125.5 2.5 broadcast_in_dim.83
  128.0 5.0 %all-to-all-start.1 = ((bf16[16,64,1024]{2,1,0:T(8,128)(2,1)}), bf16[16,64,1024]{2,1,0:T(8,128)(2,1)}, u32[]{:S(2)}, u32[]{:S(2)}) async-start(bf16[16,64,1024]{2,1,0:T(8,128)(2,1)} %broadcast_in_dim.83), calls=%async_computation.1 | async-start | bytes 4194304 | tf_op jit(solution)/shard_map/all_to_all | solution.py:56
  133.1 0.6 broadcast_multiply_fusion.1
  133.7 50.9 %all-to-all-done.1 = bf16[16,64,1024]{2,1,0:T(8,128)(2,1)} async-done(((bf16[16,64,1024]{2,1,0:T(8,128)(2,1)}), bf16[16,64,1024]{2,1,0:T(8,128)(2,1)}, u32[]{:S(2)}, u32[]{:S(2)}) %all-to-all-start.1) | async-done | bytes 2097184 | tf_op jit(solution)/shard_map/all_to_all | solution.py:56
  184.6 2.0 convert_reduce_fusion
  186.6 0.7 broadcast_multiply_fusion
  187.3 230.9 %all-gather.4.cloned.1.call-done = bf16[8192,1024]{1,0:T(8,128)(2,1)} async-done(((bf16[1024,1024]{1,0:T(8,128)(2,1)}), bf16[8192,1024]{1,0:T(8,128)(2,1)}) %all-gather.4.cloned.1.call-update) | async-done | bytes 16777232 | tf_op jit(solution)/shard_map/all_gather | solution.py:87
  418.3 15.8 %fusion.5 = f32[8192,512]{1,0:T(8,128)} fusion(bf16[8192,1024]{1,0:T(8,128)(2,1)} %all-gather.4.cloned.1.call-done, bf16[512,1024]{1,0:T(8,128)(2,1)S(1)} %copy-done), kind=kOutput, calls=%fused_computation.26 | convolution fusion | flops 8589934592 | bytes 34603008 | tf_op jit(solution)/shard_map/dot_general | solution.py:85
  434.0 9.2 %fusion = bf16[512,8192]{0,1:T(8,128)(2,1)} fusion(f32[8192,512]{1,0:T(8,128)} %fusion.5, bf16[64,512]{1,0:T(8,128)(2,1)S(1)} %convolution_convert_fusion.2, bf16[64,8192]{1,0:T(8,128)(2,1)S(1)} %bitcast.53), kind=kOutput, calls=%fused_computation.1 | convolution fusion | flops 549453824 | bytes 26279936 | tf_op jit(solution)/shard_map/dot_general | solution.py:91
  443.3 0.0 copy-start.1
  443.3 12.0 %copy.27 = bf16[512,8192]{1,0:T(8,128)(2,1)} copy(bf16[512,8192]{0,1:T(8,128)(2,1)} %fusion) | data formatting | bytes 16777216
  455.3 0.0 copy-done.1
  (5 shorter events, 0.1 us)
Async XLA Ops:
  7.2 44.3 %copy-start = (bf16[512,1024]{1,0:T(8,128)(2,1)S(1)}, bf16[512,1024]{1,0:T(8,128)(2,1)}, u32[]{:S(2)}) copy-start(bf16[512,1024]{1,0:T(8,128)(2,1)} %param.8) | copy-start | bytes 3145732
  7.2 41.8 %all-gather.6.cloned.1.call-start = ((), (), s32[]{:S(2)}) async-start(), calls=%async_computation.5 | async-start | bytes 1327104 | tf_op jit(solution)/shard_map/all_gather | solution.py:35
  9.6 408.6 %all-gather.4.cloned.1.call-start = ((), (), s32[]{:S(2)}) async-start(), calls=%async_computation.4 | async-start | bytes 18874368 | tf_op jit(solution)/shard_map/all_gather | solution.py:87
  11.2 1.0 copy-start.2
  11.2 1.3 copy-start.3
  26.8 5.0 %copy-start.5 = (f32[1024]{0:T(1024)S(1)}, f32[1024]{0:T(1024)}, u32[]{:S(2)}) copy-start(f32[1024]{0:T(1024)} %param.11) | copy-start | bytes 12292
  26.8 5.0 %copy-start.4 = (s32[16,1024]{1,0:T(8,128)S(1)}, s32[16,1024]{1,0:T(8,128)}, u32[]{:S(2)}) copy-start(s32[16,1024]{1,0:T(8,128)} %param.10) | copy-start | bytes 196612
  58.4 11.2 %all-to-all-start.2 = ((bf16[8,64,128]{2,1,0:T(8,128)(2,1)}), bf16[8,64,128]{2,1,0:T(8,128)(2,1)S(1)}, u32[]{:S(2)}, u32[]{:S(2)}) async-start(bf16[8,64,128]{2,1,0:T(8,128)(2,1)} %bitcast.51), calls=%async_computation.2 | async-start | bytes 262144 | tf_op jit(solution)/shard_map/all_to_all | solution.py:50
  69.7 30.7 %all-to-all-start = ((bf16[8,64,1024]{2,1,0:T(8,128)(2,1)}), bf16[8,64,1024]{2,1,0:T(8,128)(2,1)S(1)}, u32[]{:S(2)}, u32[]{:S(2)}) async-start(bf16[8,64,1024]{2,1,0:T(8,128)(2,1)} %bitcast.54), calls=%async_computation | async-start | bytes 2097152 | tf_op jit(solution)/shard_map/all_to_all | solution.py:50
  101.1 24.4 %all-to-all-start.3 = ((bf16[16,64,128]{2,1,0:T(8,128)(2,1)}), bf16[16,64,128]{2,1,0:T(8,128)(2,1)S(1)}, u32[]{:S(2)}, u32[]{:S(2)}) async-start(bf16[16,64,128]{2,1,0:T(8,128)(2,1)} %broadcast_in_dim.84), calls=%async_computation.3 | async-start | bytes 524288 | tf_op jit(solution)/shard_map/all_to_all | solution.py:56
  128.0 56.5 %all-to-all-start.1 = ((bf16[16,64,1024]{2,1,0:T(8,128)(2,1)}), bf16[16,64,1024]{2,1,0:T(8,128)(2,1)}, u32[]{:S(2)}, u32[]{:S(2)}) async-start(bf16[16,64,1024]{2,1,0:T(8,128)(2,1)} %broadcast_in_dim.83), calls=%async_computation.1 | async-start | bytes 4194304 | tf_op jit(solution)/shard_map/all_to_all | solution.py:56
  443.3 12.0 %copy-start.1 = (bf16[512,1024]{1,0:T(8,128)(2,1)S(1)}, bf16[512,1024]{1,0:T(8,128)(2,1)}, u32[]{:S(2)}) copy-start(bf16[512,1024]{1,0:T(8,128)(2,1)} %param.8) | copy-start | bytes 3145732
Sparse Core Ops, SparseCore 0:
  10.2 38.7 all-gather.5
  51.2 367.0 all-gather.3
where the time goes:
time: 463 us; the launch traced here: 462 us
  waiting for transfers between devices  321 us (69%)
  local copies, waits for them, and re-layouts  43.1 us (9%)
  matrix products  37.4 us (8%)
  starting transfers between devices  26.7 us (6%)
  other arithmetic  19.5 us (4%)
  between operations  14.2 us (3%)
    all_gather x1, waiting for transfers between devices, local(): lax.all_gather(local_rows, 'fsdp', axis=0, tiled=True)  231 us
    all_to_all x2, waiting for transfers between devices, copy_for_each(): lax.all_to_all(jnp.broadcast_to(value[None], (length, *value.shape)), axi...  62 us
    all_to_all x2, waiting for transfers between devices, sum_at_owner(): lax.all_to_all(tiles, axis, split_axis=0, concat_axis=0, tiled=True)  25.6 us
    all_to_all x2, starting transfers between devices, copy_for_each(): lax.all_to_all(jnp.broadcast_to(value[None], (length, *value.shape)), axi...  17.4 us
    dot_general x1, matrix products, local(): lax.dot_general(grad_out, lax.all_gather(local_rows, 'fsdp', axis=0, tile...  15.8 us
    unnamed x15, local copies, waits for them, and re-layouts  14.9 us
    select_n x2, local copies, waits for them, and re-layouts, dequantize(): levels = jnp.where(nibbles == position, jnp.float32(quantum), levels)  10.2 us
  transfers between devices with their start and end apart: 6, of which 5 were waited for; matrix products, arithmetic and copies ran while one was open for 13% of the time, Pallas kernels for 0%

commit v1 on v0

v1 whole, which is shorter than its diff:
```python
import functools

import jax
import jax.numpy as jnp
from jax import lax
from jax.experimental import pallas as pl
from jax.experimental.pallas import tpu as pltpu
from jax.sharding import Mesh
from jax.sharding import PartitionSpec as P


adapter_scale = 0.5
nf4_table = [
    -1.0,
    -0.6961928009986877,
    -0.5250730514526367,
    -0.39491748809814453,
    -0.28444138169288635,
    -0.18477343022823334,
    -0.09105003625154495,
    0.0,
    0.07958029955625534,
    0.16093020141124725,
    0.24611230194568634,
    0.33791524171829224,
    0.44070982933044434,
    0.5626170039176941,
    0.7229568362236023,
    1.0,
]

AXES = ("y", "xh", "core", "z", "xl")
SIZES = (4, 2, 2, 4, 2)
DEVICES = 128
HALF = 512
SHARD = 1024
WIDTH = 8192
COLS = 1024
TOKENS = 512
RANK_HALF = 32
UP = 128
PACKED = 1152


def place(device):
    rest, xl = divmod(device, 2)
    rest, z = divmod(rest, 4)
    rest, core = divmod(rest, 2)
    y, xh = divmod(rest, 2)
    return xh * 2 + xl, y, z, core


def device_at(x, y, z, core):
    return (((y * 2 + x // 2) * 2 + core) * 4 + z) * 2 + x % 2


def z_hop(x, y, z, core):
    step = 1 if (core + y) % 2 == 0 else -1
    return x, y, (z + step) % 4, core


def x_hop(x, y, z, core):
    step = 1 if core == 0 else -1
    return (x + step) % 4, y, z, core


def y_swap(x, y, z, core):
    step = 1 if (core + y) % 2 == 0 else -1
    return x, (y + step) % 4, z, core


def core_swap(x, y, z, core):
    return x, y, z, 1 - core


def moved(value, hop):
    pairs = [(d, device_at(*hop(*place(d)))) for d in range(DEVICES)]
    return lax.ppermute(value, AXES, pairs)


NT = (((1,), (1,)), ((), ()))
TN = (((0,), (0,)), ((), ()))
VMEM = pl.BlockSpec(memory_space=pltpu.VMEM)
ANY = pl.BlockSpec(memory_space=pl.ANY)
HBM = pl.BlockSpec(memory_space=pltpu.HBM)


def position():
    y, core, z, xl = (lax.axis_index(name) for name in ("y", "core", "z", "xl"))
    return y, core, z, xl


def piece_place(slot):
    y, core, _, _ = position()
    half = core if slot < 8 else 1 - core
    step = 1 - 2 * lax.rem(half + y, 2)
    ups = (0, -step, 0, 2, -step, step, 2, step)
    crosses = (0, 0, 1, 0, 1, 0, 1, 1)
    return lax.rem(ups[slot % 8] + 4, 4), crosses[slot % 8], half


def shard_at(up, cross):
    _, _, z, xl = position()
    return lax.rem(z + up, 4) * 2 + lax.rem(xl + cross, 2)


def pack_kernel(down_ref, up_ref, packed_ref):
    _, core, _, _ = position()
    ranks = pl.ds(pl.multiple_of(core * RANK_HALF, RANK_HALF), RANK_HALF)
    packed_ref[:, :SHARD] = down_ref[ranks, :]
    packed_ref[:, SHARD:] = up_ref[ranks, :]


def packed_half(down_adapter, up_adapter):
    return pl.pallas_call(
        pack_kernel,
        in_specs=[VMEM, VMEM],
        out_specs=VMEM,
        out_shape=pltpu.VMEM((RANK_HALF, PACKED), jnp.bfloat16),
        compiler_params=LIMIT,
        name="pack",
    )(down_adapter, up_adapter)


def join_kernel(mine_ref, crossed_ref, pair_ref):
    pair_ref[0] = mine_ref[...]
    pair_ref[1] = crossed_ref[...]


def joined(mine, crossed):
    return pl.pallas_call(
        join_kernel,
        in_specs=[VMEM, VMEM],
        out_specs=VMEM,
        out_shape=pltpu.VMEM((2, RANK_HALF, PACKED), jnp.bfloat16),
        compiler_params=LIMIT,
        name="join",
    )(in_vmem(mine), in_vmem(crossed))


def prepare_kernel(
    codes_ref, scale_ref, col_ref, acts_ref,
    weight_ref, held_ref, words_ref, scales_ref, rows_ref, arrived
):
    _, core, _, _ = position()
    first = pl.multiple_of(core * 8, 8)
    scales = pltpu.make_async_copy(scale_ref.at[pl.ds(first, 8)], scales_ref, arrived.at[0])
    words = [
        pltpu.make_async_copy(
            codes_ref.at[pl.ds(first + 2 * i, 2)], words_ref.at[pl.ds(2 * i, 2)], arrived.at[1 + i]
        )
        for i in range(4)
    ]
    scales.start()
    for copy in words:
        copy.start()
    acts = [
        pltpu.make_async_copy(
            acts_ref.at[i * 64 : (i + 1) * 64], held_ref.at[i * 64 : (i + 1) * 64], arrived.at[5 + i]
        )
        for i in range(8)
    ]
    scales.wait()
    for copy in acts:
        copy.start()

    def block(b):
        absmax = scales_ref[pl.ds(b, 1), :].astype(jnp.float32)
        absmax = (absmax + 1.0) / 256.0 * col_ref[...]
        for lane in range(COLS // 128):
            code = words_ref[b, :, lane * 128 : (lane + 1) * 128]
            scale = absmax[:, lane * 128 : (lane + 1) * 128]
            for j in range(4):
                bits = [(code & (1 << (4 * j + k))) != 0 for k in range(4)]
                levels = [jnp.full(code.shape, q, jnp.float32) for q in nf4_table]
                for k in range(4):
                    levels = [
                        jnp.where(bits[k], levels[i + 1], levels[i])
                        for i in range(0, len(levels), 2)
                    ]
                rows_ref[lane, pl.ds(j, 16, stride=4), :] = levels[0] * scale
        for lane in range(COLS // 128):
            weight_ref[pl.ds(pl.multiple_of(b * 64, 64), 64), lane * 128 : (lane + 1) * 128] = (
                rows_ref[lane].astype(jnp.bfloat16)
            )

    for copy in words:
        copy.wait()
    pl.loop(0, 8)(block)
    for copy in acts:
        copy.wait()


def prepared(codes, scale_codes, col_scale, acts):
    return pl.pallas_call(
        prepare_kernel,
        in_specs=[HBM, HBM, VMEM, HBM],
        out_specs=[VMEM, VMEM],
        out_shape=[
            pltpu.VMEM((HALF, COLS), jnp.bfloat16),
            pltpu.VMEM((TOKENS, WIDTH), jnp.bfloat16),
        ],
        scratch_shapes=[
            pltpu.VMEM((8, 16, COLS), jnp.int32),
            pltpu.VMEM((8, COLS), jnp.int32),
            pltpu.VMEM((COLS // 128, 64, 128), jnp.float32),
            pltpu.SemaphoreType.DMA((13,)),
        ],
        compiler_params=LIMIT,
        cost_estimate=pl.CostEstimate(
            flops=2_000_000_000, bytes_accessed=9_600_000, transcendentals=0
        ),
        name="prepare",
    )(in_hbm(codes), in_hbm(scale_codes), col_scale.reshape(1, COLS), in_hbm(acts))


def in_hbm(value):
    return pltpu.with_memory_space_constraint(value, pltpu.HBM)


def in_vmem(value):
    return pltpu.with_memory_space_constraint(value, pltpu.VMEM)


LIMIT = pltpu.CompilerParams(vmem_limit_bytes=12 * 2**20)


def adapter_kernel(grad_ref, *refs):
    own_refs, other_refs = refs[:4], refs[4:8]
    acts_ref, mixed_ref, down_ref, sums_ref, rest_ref = refs[8:]
    order = [(up, cross) for up in range(4) for cross in range(2)]

    def columns(up, cross, width):
        return pl.ds(pl.multiple_of(shard_at(up, cross) * width, width), width)

    mixed = jnp.zeros((TOKENS, 2 * RANK_HALF), jnp.float32)
    for up, cross in order:
        down_ref[up, cross, :RANK_HALF] = own_refs[up][cross, :, :SHARD]
        down_ref[up, cross, RANK_HALF:] = other_refs[up][cross, :, :SHARD]
        up_rows = jnp.concatenate(
            [own_refs[up][cross, :, SHARD:], other_refs[up][cross, :, SHARD:]], axis=0
        )
        mixed += lax.dot_general(
            grad_ref[:, columns(up, cross, UP)], up_rows, NT, preferred_element_type=jnp.float32
        )
    mixed = mixed.astype(jnp.bfloat16)
    mixed_ref[...] = mixed

    lowered = jnp.zeros((TOKENS, 2 * RANK_HALF), jnp.float32)
    for up, cross in order:
        acts = acts_ref[:, columns(up, cross, SHARD)]
        term = lax.dot_general(mixed, acts, TN, preferred_element_type=jnp.float32)
        lowered += lax.dot_general(
            acts, down_ref[up, cross], NT, preferred_element_type=jnp.float32
        )
        sums_ref[up, cross, :, :SHARD] = term[:RANK_HALF].astype(jnp.bfloat16)
        rest_ref[up, cross, :, :SHARD] = term[RANK_HALF:].astype(jnp.bfloat16)
    lowered = lowered.astype(jnp.bfloat16)
    for up, cross in order:
        term = lax.dot_general(
            lowered, grad_ref[:, columns(up, cross, UP)], TN, preferred_element_type=jnp.float32
        ).astype(jnp.bfloat16)
        sums_ref[up, cross, :, SHARD:] = term[:RANK_HALF]
        rest_ref[up, cross, :, SHARD:] = term[RANK_HALF:]


def adapter_terms(grad_out, own, other, acts):
    packed = pltpu.VMEM((4, 2, RANK_HALF, PACKED), jnp.bfloat16)
    return pl.pallas_call(
        adapter_kernel,
        in_specs=[VMEM] * 10,
        out_specs=[VMEM] * 4,
        out_shape=[
            pltpu.VMEM((TOKENS, 2 * RANK_HALF), jnp.bfloat16),
            pltpu.VMEM((4, 2, 2 * RANK_HALF, SHARD), jnp.bfloat16),
            packed,
            packed,
        ],
        compiler_params=LIMIT,
        cost_estimate=pl.CostEstimate(
            flops=5_000_000_000, bytes_accessed=12_000_000, transcendentals=0
        ),
        name="adapter",
    )(*map(in_vmem, (grad_out, *own, *other, acts)))


def two_sums_kernel(mine_ref, arrived_ref, *out_refs):
    for i, ref in enumerate(out_refs):
        ref[...] = (
            mine_ref[i].astype(jnp.float32) + arrived_ref[i].astype(jnp.float32)
        ).astype(jnp.bfloat16)


def core_sums(mine, arrived):
    shape = pltpu.VMEM((2, RANK_HALF, PACKED), jnp.bfloat16)
    return pl.pallas_call(
        two_sums_kernel,
        in_specs=[VMEM, VMEM],
        out_specs=[VMEM] * 4,
        out_shape=[shape] * 4,
        compiler_params=LIMIT,
        name="core_sums",
    )(in_vmem(mine), in_vmem(arrived))


def four_sums_kernel(split, scale, *refs):
    ins, outs = refs[:4], refs[4:]
    total = ins[0][...].astype(jnp.float32)
    for ref in ins[1:]:
        total += ref[...].astype(jnp.float32)
    if scale is not None:
        total = total * scale
    for i, ref in enumerate(outs):
        ref[...] = (total[i] if split else total).astype(ref.dtype)


def four_sums(parts, split, dtype, scale=None):
    shape = pltpu.VMEM((RANK_HALF, PACKED), dtype)
    return pl.pallas_call(
        functools.partial(four_sums_kernel, split, scale),
        in_specs=[VMEM] * 4,
        out_specs=[VMEM] * 2 if split else VMEM,
        out_shape=[shape] * 2 if split else shape,
        compiler_params=LIMIT,
    )(*map(in_vmem, parts))


def product_kernel(slots, aliased, *refs):
    count = len(slots)
    weights, refs = refs[:count], refs[count:]
    grad_ref, mixed_ref, down_ref = refs[:3]
    refs = refs[4:] if aliased else refs[3:]
    out_ref, made_ref, sent = refs

    def copy(k):
        up, cross, half = piece_place(slots[k])
        column = pl.multiple_of((shard_at(up, cross) * 2 + half) * HALF, HALF)
        return pltpu.make_async_copy(
            made_ref.at[k % 2], out_ref.at[:, pl.ds(column, HALF)], sent.at[k % 2]
        )

    for k in range(count):
        up, cross, half = piece_place(slots[k])
        down = down_ref[up, cross, :, pl.ds(pl.multiple_of(half * HALF, HALF), HALF)]
        side = jnp.dot(mixed_ref[...], down, preferred_element_type=jnp.float32)
        base = lax.dot_general(
            grad_ref[...], weights[k][...], NT, preferred_element_type=jnp.float32
        )
        if k >= 2:
            copy(k - 2).wait()
        made_ref[k % 2] = (base + adapter_scale * side).astype(jnp.bfloat16)
        copy(k).start()
    for k in range(max(0, count - 2), count):
        copy(k).wait()


def product(slots, weights, grad_out, mixed, down, target):
    count, aliased = len(weights), target is not None
    return pl.pallas_call(
        functools.partial(product_kernel, slots, aliased),
        in_specs=[VMEM] * (count + 3) + [ANY] * aliased,
        out_specs=ANY,
        out_shape=jax.ShapeDtypeStruct((TOKENS, WIDTH), jnp.bfloat16),
        scratch_shapes=[
            pltpu.VMEM((2, TOKENS, HALF), jnp.bfloat16),
            pltpu.SemaphoreType.DMA((2,)),
        ],
        input_output_aliases={count + 3: 0} if aliased else {},
        cost_estimate=pl.CostEstimate(
            flops=2 * count * TOKENS * HALF * 1100,
            bytes_accessed=count * 1_600_000 + 1_000_000,
            transcendentals=0,
        ),
        compiler_params=LIMIT,
    )(*map(in_vmem, (*weights, grad_out, mixed, down)), *([target] if aliased else []))


def final_kernel(mine_ref, theirs_ref, down_ref, up_ref):
    _, core, _, _ = position()
    for ref, half in ((mine_ref, core), (theirs_ref, 1 - core)):
        rows = pl.ds(pl.multiple_of(half * RANK_HALF, RANK_HALF), RANK_HALF)
        down_ref[rows, :] = ref[:, :SHARD]
        up_ref[rows, :] = ref[:, SHARD:]


def in_order(mine, theirs):
    return pl.pallas_call(
        final_kernel,
        in_specs=[VMEM, VMEM],
        out_specs=[VMEM, VMEM],
        out_shape=[
            jax.ShapeDtypeStruct((2 * RANK_HALF, SHARD), jnp.float32),
            jax.ShapeDtypeStruct((2 * RANK_HALF, UP), jnp.float32),
        ],
        compiler_params=LIMIT,
        name="in_order",
    )(in_vmem(mine), in_vmem(theirs))


def shifted(axis, by):
    def hop(*at):
        at = list(at)
        at["xyz".index(axis)] = (at["xyz".index(axis)] + by) % 4
        return tuple(at)

    return hop


def step(acts, grad_out, codes, scale_codes, col_scale, down_adapter, up_adapter):
    packed = packed_half(down_adapter, up_adapter)
    crossed = moved(packed, x_hop)
    w, acts = prepared(codes, scale_codes, col_scale, acts)
    pair = joined(packed, crossed)
    own, other = [pair] + [None] * 3, [None] * 4
    for dz in (1, 3, 2):
        own[4 - dz] = moved(pair, shifted("z", dz))
    for up in (0, 3, 1, 2):
        other[up] = moved(own[up], core_swap)
    w_z1 = moved(w, z_hop)
    w_x0 = moved(w, x_hop)
    w_z2 = moved(w_z1, z_hop)
    w_x1 = moved(w_z1, x_hop)
    w_y1 = moved(w_z1, y_swap)
    w_x2 = moved(w_z2, x_hop)
    w_xy = moved(w_x1, y_swap)

    mixed, down, sums, rest = adapter_terms(grad_out, own, other, acts)
    arrived = moved(rest, core_swap)
    sums = core_sums(sums, arrived)
    parts = [sums[0]]
    for dz in (1, 3, 2):
        parts.append(moved(sums[dz], shifted("z", dz)))
    mine, cross = four_sums(parts, True, jnp.bfloat16)
    parts = [mine]
    for dx, part in ((1, cross), (3, cross), (2, mine)):
        parts.append(moved(part, shifted("x", dx)))
    mine = four_sums(parts, False, jnp.bfloat16)
    parts = [mine]
    for dy in (1, 3, 2):
        parts.append(moved(mine, shifted("y", dy)))
    scale = adapter_scale * float(TOKENS * DEVICES) ** (-0.5)
    mine = four_sums(parts, False, jnp.float32, scale)

    pieces = (w, w_z1, w_x0, w_z2, w_x1, w_y1, w_x2, w_xy)
    mirrored = []
    for piece in pieces:
        mirrored.append(moved(piece, core_swap))
    out = None
    for stage in ((0,), (1, 2), (3, 4, 5), (6, 7)):
        slots = stage + tuple(8 + k for k in stage)
        weights = [pieces[k] for k in stage] + [mirrored[k] for k in stage]
        out = product(slots, weights, grad_out, mixed, down, out)

    theirs = moved(mine, core_swap)
    grad_down, grad_up = in_order(mine, theirs)
    return out, grad_down, grad_up


def solution(mesh):
    fine = Mesh(mesh.devices.reshape(SIZES), AXES)
    fsdp = ("z", "xl")
    placed = (
        P(AXES, None),
        P(AXES, None),
        P(fsdp, None, None),
        P(fsdp, None),
        P(),
        P(None, fsdp),
        P(None, fsdp),
    )
    return jax.shard_map(
        step,
        mesh=fine,
        in_specs=placed,
        out_specs=(P(AXES, None), P(None, fsdp), P(None, fsdp)),
        check_vma=False,
    )
```

time: 463 us -> 136 us (0.29)
  waiting for transfers between devices: 321 us -> 48.4 us
  local copies, waits for them, and re-layouts: 43.1 us -> 2.3 us
  matrix products: 37.4 us -> 0 us
  starting transfers between devices: 26.7 us -> 56.6 us
  Pallas kernels: 0 us -> 27.7 us
  other arithmetic: 19.5 us -> 0 us
  between operations: 14.2 us -> 0.98 us
    all_gather x2 -> x0, waiting for transfers between devices: 234 us -> none  [the longest x1 231 us: local(): lax.all_gather(local_rows, 'fsdp', axis=0, tiled=True)]
    all_to_all x4 -> x0, waiting for transfers between devices: 87.6 us -> none  [the longest x2 62 us: copy_for_each(): lax.all_to_all(jnp.broadcast_to(value[None], (length, *value.shape)), axi...]
    ppermute x0 -> x34, starting transfers between devices: none -> 56.6 us  [moved(): return lax.ppermute(value, AXES, pairs)]
    ppermute x0 -> x34, waiting for transfers between devices: none -> 48.4 us  [moved(): return lax.ppermute(value, AXES, pairs)]
    dot_general x5 -> x0, matrix products: 37.4 us -> none  [the longest x1 15.8 us: local(): lax.dot_general(grad_out, lax.all_gather(local_rows, 'fsdp', axis=0, tile...]
    pallas_call x0 -> x13, Pallas kernels: none -> 27.7 us  [the longest x4 17.5 us: product(): pl.pallas_call(functools.partial(product_kernel, slots, aliased), in_spec...]
    all_to_all x4 -> x0, starting transfers between devices: 26.6 us -> none  [the longest x2 17.4 us: copy_for_each(): lax.all_to_all(jnp.broadcast_to(value[None], (length, *value.shape)), axi...]
    unnamed x15 -> x8, local copies, waits for them, and re-layouts: 14.9 us -> 2.3 us
  transfers between devices with their start and end apart: 6 -> 34, of which waited for: 5 -> 14; matrix products, arithmetic and copies ran while one was open for 13% -> 0% of each run, Pallas kernels for 0% -> 17%
where the time goes in v1:
time: 136 us
  starting transfers between devices  56.6 us (42%)
  waiting for transfers between devices  48.4 us (36%)
  Pallas kernels  27.7 us (20%)
  local copies, waits for them, and re-layouts  2.3 us (2%)
    ppermute x34, starting transfers between devices, moved(): return lax.ppermute(value, AXES, pairs)  56.6 us
    ppermute x34, waiting for transfers between devices, moved(): return lax.ppermute(value, AXES, pairs)  48.4 us
    pallas_call x4, Pallas kernels, product(): pl.pallas_call(functools.partial(product_kernel, slots, aliased), in_spec...  17.5 us
    pallas_call x1, Pallas kernels, adapter_terms(): pl.pallas_call(adapter_kernel, in_specs=[VMEM] * 10, out_specs=[VMEM] * 4...  4.89 us
    pallas_call x1, Pallas kernels, prepared(): pl.pallas_call(prepare_kernel, in_specs=[HBM, HBM, VMEM, HBM], out_specs=...  4.32 us
  transfers between devices with their start and end apart: 34, of which 14 were waited for; matrix products, arithmetic and copies ran while one was open for 0% of the time, Pallas kernels for 17%

profile of v1, /device:TPU:1, one launch (start us, length us, event | category | flops | bytes accessed | tf_op | source)
XLA Modules:
  0.0 135.9 jit_solution(4879245981372299423)
XLA Ops:
  0.6 0.9 copy-done.1
  1.5 0.7 copy-done.2
  2.3 3.4 %collective-permute-start.7 = (bf16[32,1152]{1,0:T(8,128)(2,1)S(1)}, bf16[32,1152]{1,0:T(8,128)(2,1)S(1)}, u32[]{:S(2)}, u32[]{:S(2)}) collective-permute-start(bf16[32,1152]{1,0:T(8,128)(2,1)S(1)} %pack.1.mine_ref), channel_id=1, source_target_pairs={{0,1},{1,16},{2,3},{3,18},{4,5},{5,20},{6,7},{7,22},{8,25},{9,8},{... | collective-permute-start | bytes 221192 | tf_op jit(solution)/shard_map/ppermute | solution.py:78
  5.6 1.4 %collective-permute-done.7.crossed_ref = bf16[32,1152]{1,0:T(8,128)(2,1)S(1)} collective-permute-done((bf16[32,1152]{1,0:T(8,128)(2,1)S(1)}, bf16[32,1152]{1,0:T(8,128)(2,1)S(1)}, u32[]{:S(2)}, u32[]{:S(2)}) %collective-permute-start.7) | collective-permute-done | bytes 73760 | tf_op jit(solution)/shard_map/ppermute | solution.py:78
  7.1 3.8 %collective-permute-start.8 = (bf16[2,32,1152]{2,1,0:T(8,128)(2,1)S(1)}, bf16[2,32,1152]{2,1,0:T(8,128)(2,1)S(1)}, u32[]{:S(2)}, u32[]{:S(2)}) collective-permute-start(bf16[2,32,1152]{2,1,0:T(8,128)(2,1)S(1)} %join.1.refs_0_), channel_id=1, source_target_pairs={{0,6},{1,7},{2,0},{3,1},{4,2},{5,3},{6,4},{7,5},{8,14},{9,15},{10,... | collective-permute-start | bytes 442376 | tf_op jit(solution)/shard_map/ppermute | solution.py:78
  10.9 0.7 collective-permute-start.10
  11.6 3.2 %collective-permute-start.11 = (bf16[2,32,1152]{2,1,0:T(8,128)(2,1)S(1)}, bf16[2,32,1152]{2,1,0:T(8,128)(2,1)S(1)}, u32[]{:S(2)}, u32[]{:S(2)}) collective-permute-start(bf16[2,32,1152]{2,1,0:T(8,128)(2,1)S(1)} %join.1.refs_0_), channel_id=1, source_target_pairs={{0,8},{1,9},{2,10},{3,11},{4,12},{5,13},{6,14},{7,15},{8,0},{9,1},... | collective-permute-start | bytes 442376 | tf_op jit(solution)/shard_map/ppermute | solution.py:78
  14.8 0.0 collective-permute-done.8.refs_1_
  14.8 3.4 %collective-permute-start.12 = (bf16[2,32,1152]{2,1,0:T(8,128)(2,1)S(1)}, bf16[2,32,1152]{2,1,0:T(8,128)(2,1)S(1)}, u32[]{:S(2)}, u32[]{:S(2)}) collective-permute-start(bf16[2,32,1152]{2,1,0:T(8,128)(2,1)S(1)} %collective-permute-done.8.refs_1_), channel_id=1, source_target_pairs={{0,8},{1,9},{2,10},{3,11},{4,12},{5,13},{6,14},{7,15},{8,0},{9,1},... | collective-permute-start | bytes 442376 | tf_op jit(solution)/shard_map/ppermute | solution.py:78
  18.1 2.2 %collective-permute-start.13 = (bf16[2,32,1152]{2,1,0:T(8,128)(2,1)S(1)}, bf16[2,32,1152]{2,1,0:T(8,128)(2,1)S(1)}, u32[]{:S(2)}, u32[]{:S(2)}) collective-permute-start(bf16[2,32,1152]{2,1,0:T(8,128)(2,1)S(1)} %collective-permute-done.9.refs_2_), channel_id=1, source_target_pairs={{0,8},{1,9},{2,10},{3,11},{4,12},{5,13},{6,14},{7,15},{8,0},{9,1},... | collective-permute-start | bytes 442376 | tf_op jit(solution)/shard_map/ppermute | solution.py:78
  20.4 1.1 collective-permute-start.14
  21.5 0.7 copy-done.3
  22.2 4.3 %prepare.1 = (bf16[512,1024]{1,0:T(8,128)(2,1)S(1)}, bf16[512,8192]{1,0:T(8,128)(2,1)S(1)}) custom-call(s32[16,16,1024]{2,1,0:T(8,128)} %codes_ref.1, s32[16,1024]{1,0:T(8,128)} %scale_ref.1, f32[1,1024]{1,0:T(1,128)S(1)} %bitcast.1, bf16[512,8192]{1,0:T(8,128)(2,1)} %acts_ref.1), custom_call_target="tpu_custom_call" | custom-call | flops 2000000000 | bytes 9600000 | tf_op jit(solution)/shard_map/prepare/pallas_call | solution.py:195
  26.5 0.7 collective-permute-start
  27.3 0.0 collective-permute-done.14.refs_7_
  27.3 4.9 %adapter.1 = (bf16[512,64]{1,0:T(8,128)(2,1)S(1)}, bf16[4,2,64,1024]{3,2,1,0:T(8,128)(2,1)S(1)}, bf16[4,2,32,1152]{3,2,1,0:T(8,128)(2,1)S(1)}, bf16[4,2,32,1152]{3,2,1,0:T(8,128)(2,1)S(1)}) custom-call(bf16[512,1024]{1,0:T(8,128)(2,1)S(1)} %copy-done, bf16[2,32,1152]{2,1,0:T(8,128)(2,1)S(1)} %join.1.refs_0_, ...), custom_call_target="tpu_custom_call" | custom-call | flops 5000000000 | bytes 12000000 | tf_op jit(solution)/shard_map/adapter/pallas_call | solution.py:269
  32.2 0.1 collective-permute-start.23
  32.3 0.5 collective-permute-start.22
  32.8 3.0 %collective-permute-start.19 = (bf16[512,1024]{1,0:T(8,128)(2,1)S(1)}, bf16[512,1024]{1,0:T(8,128)(2,1)S(1)}, u32[]{:S(2)}, u32[]{:S(2)}) collective-permute-start(bf16[512,1024]{1,0:T(8,128)(2,1)S(1)} %get-tuple-element.17.refs_0_), channel_id=1, source_target_pairs={{0,1},{1,16},{2,3},{3,18},{4,5},{5,20},{6,7},{7,22},{8,25},{9,8},{... | collective-permute-start | bytes 3145736 | tf_op jit(solution)/shard_map/ppermute | solution.py:78
  35.8 0.0 collective-permute-done.23.arrived_ref
  35.8 0.1 core_sums.1
  35.9 0.9 collective-permute-start.24
  36.8 1.8 %collective-permute-start.25 = (bf16[2,32,1152]{2,1,0:T(8,128)(2,1)S(1)}, bf16[2,32,1152]{2,1,0:T(8,128)(2,1)S(1)}, u32[]{:S(2)}, u32[]{:S(2)}) collective-permute-start(bf16[2,32,1152]{2,1,0:T(8,128)(2,1)S(1)} %get-tuple-element.25), channel_id=1, source_target_pairs={{0,6},{1,7},{2,0},{3,1},{4,2},{5,3},{6,4},{7,5},{8,14},{9,15},{10,... | collective-permute-start | bytes 442376 | tf_op jit(solution)/shard_map/ppermute | solution.py:78
  38.6 3.5 %collective-permute-done.refs_0_ = bf16[512,1024]{1,0:T(8,128)(2,1)S(1)} collective-permute-done((bf16[512,1024]{1,0:T(8,128)(2,1)S(1)}, bf16[512,1024]{1,0:T(8,128)(2,1)S(1)}, u32[]{:S(2)}, u32[]{:S(2)}) %collective-permute-start) | collective-permute-done | bytes 1048608 | tf_op jit(solution)/shard_map/ppermute | solution.py:78
  42.1 0.0 collective-permute-start.26
  42.1 0.9 collective-permute-done.24.refs_1_
  43.0 0.8 collective-permute-start.1
  43.9 0.0 collective-permute-done.25.refs_2_
  43.9 3.0 %collective-permute-start.3 = (bf16[512,1024]{1,0:T(8,128)(2,1)S(1)}, bf16[512,1024]{1,0:T(8,128)(2,1)S(1)}, u32[]{:S(2)}, u32[]{:S(2)}) collective-permute-start(bf16[512,1024]{1,0:T(8,128)(2,1)S(1)} %collective-permute-done.refs_0_), channel_id=1, source_target_pairs={{0,1},{1,16},{2,3},{3,18},{4,5},{5,20},{6,7},{7,22},{8,25},{9,8},{... | collective-permute-start | bytes 3145736 | tf_op jit(solution)/shard_map/ppermute | solution.py:78
  46.9 0.7 collective-permute-done.26.refs_3_
  47.6 0.1 shard_map.98
  47.7 0.6 collective-permute-start.27
  48.3 5.3 %collective-permute-done.27.refs_1_ = bf16[32,1152]{1,0:T(8,128)(2,1)S(1)} collective-permute-done((bf16[32,1152]{1,0:T(8,128)(2,1)S(1)}, bf16[32,1152]{1,0:T(8,128)(2,1)S(1)}, u32[]{:S(2)}, u32[]{:S(2)}) %collective-permute-start.27) | collective-permute-done | bytes 73760 | tf_op jit(solution)/shard_map/ppermute | solution.py:78
  53.6 1.5 %collective-permute-start.28 = (bf16[32,1152]{1,0:T(8,128)(2,1)S(1)}, bf16[32,1152]{1,0:T(8,128)(2,1)S(1)}, u32[]{:S(2)}, u32[]{:S(2)}) collective-permute-start(bf16[32,1152]{1,0:T(8,128)(2,1)S(1)} %get-tuple-element.28), channel_id=1, source_target_pairs={{0,17},{1,0},{2,19},{3,2},{4,21},{5,4},{6,23},{7,6},{8,25},{9,8},{... | collective-permute-start | bytes 221192 | tf_op jit(solution)/shard_map/ppermute | solution.py:78
  55.1 4.5 %collective-permute-done.28.refs_2_ = bf16[32,1152]{1,0:T(8,128)(2,1)S(1)} collective-permute-done((bf16[32,1152]{1,0:T(8,128)(2,1)S(1)}, bf16[32,1152]{1,0:T(8,128)(2,1)S(1)}, u32[]{:S(2)}, u32[]{:S(2)}) %collective-permute-start.28) | collective-permute-done | bytes 73760 | tf_op jit(solution)/shard_map/ppermute | solution.py:78
  59.5 1.9 %collective-permute-start.29 = (bf16[32,1152]{1,0:T(8,128)(2,1)S(1)}, bf16[32,1152]{1,0:T(8,128)(2,1)S(1)}, u32[]{:S(2)}, u32[]{:S(2)}) collective-permute-start(bf16[32,1152]{1,0:T(8,128)(2,1)S(1)} %get-tuple-element.27.refs_0_), channel_id=1, source_target_pairs={{0,16},{1,17},{2,18},{3,19},{4,20},{5,21},{6,22},{7,23},{8,24},{9,... | collective-permute-start | bytes 221192 | tf_op jit(solution)/shard_map/ppermute | solution.py:78
  61.4 3.5 %collective-permute-done.29.refs_3_ = bf16[32,1152]{1,0:T(8,128)(2,1)S(1)} collective-permute-done((bf16[32,1152]{1,0:T(8,128)(2,1)S(1)}, bf16[32,1152]{1,0:T(8,128)(2,1)S(1)}, u32[]{:S(2)}, u32[]{:S(2)}) %collective-permute-start.29) | collective-permute-done | bytes 73760 | tf_op jit(solution)/shard_map/ppermute | solution.py:78
  65.0 1.3 collective-permute-start.30
  66.3 3.2 %collective-permute-done.30.refs_1_ = bf16[32,1152]{1,0:T(8,128)(2,1)S(1)} collective-permute-done((bf16[32,1152]{1,0:T(8,128)(2,1)S(1)}, bf16[32,1152]{1,0:T(8,128)(2,1)S(1)}, u32[]{:S(2)}, u32[]{:S(2)}) %collective-permute-start.30) | collective-permute-done | bytes 73760 | tf_op jit(solution)/shard_map/ppermute | solution.py:78
  69.5 1.4 %collective-permute-start.31 = (bf16[32,1152]{1,0:T(8,128)(2,1)S(1)}, bf16[32,1152]{1,0:T(8,128)(2,1)S(1)}, u32[]{:S(2)}, u32[]{:S(2)}) collective-permute-start(bf16[32,1152]{1,0:T(8,128)(2,1)S(1)} %shard_map.99.refs_0_), channel_id=1, source_target_pairs={{0,96},{1,97},{2,98},{3,99},{4,100},{5,101},{6,102},{7,103},{8,104... | collective-permute-start | bytes 221192 | tf_op jit(solution)/shard_map/ppermute | solution.py:78
  70.9 2.1 %collective-permute-done.31.refs_2_ = bf16[32,1152]{1,0:T(8,128)(2,1)S(1)} collective-permute-done((bf16[32,1152]{1,0:T(8,128)(2,1)S(1)}, bf16[32,1152]{1,0:T(8,128)(2,1)S(1)}, u32[]{:S(2)}, u32[]{:S(2)}) %collective-permute-start.31) | collective-permute-done | bytes 73760 | tf_op jit(solution)/shard_map/ppermute | solution.py:78
  73.0 1.4 %collective-permute-start.32 = (bf16[32,1152]{1,0:T(8,128)(2,1)S(1)}, bf16[32,1152]{1,0:T(8,128)(2,1)S(1)}, u32[]{:S(2)}, u32[]{:S(2)}) collective-permute-start(bf16[32,1152]{1,0:T(8,128)(2,1)S(1)} %shard_map.99.refs_0_), channel_id=1, source_target_pairs={{0,64},{1,65},{2,66},{3,67},{4,68},{5,69},{6,70},{7,71},{8,72},{9,... | collective-permute-start | bytes 221192 | tf_op jit(solution)/shard_map/ppermute | solution.py:78
  74.4 3.3 %collective-permute-done.32.refs_3_ = bf16[32,1152]{1,0:T(8,128)(2,1)S(1)} collective-permute-done((bf16[32,1152]{1,0:T(8,128)(2,1)S(1)}, bf16[32,1152]{1,0:T(8,128)(2,1)S(1)}, u32[]{:S(2)}, u32[]{:S(2)}) %collective-permute-start.32) | collective-permute-done | bytes 73760 | tf_op jit(solution)/shard_map/ppermute | solution.py:78
  77.8 12.3 %collective-permute-start.33 = (f32[32,1152]{1,0:T(8,128)S(1)}, f32[32,1152]{1,0:T(8,128)S(1)}, u32[]{:S(2)}, u32[]{:S(2)}) collective-permute-start(f32[32,1152]{1,0:T(8,128)S(1)} %shard_map.100.mine_ref), channel_id=1, source_target_pairs={{0,8},{1,9},{2,10},{3,11},{4,12},{5,13},{6,14},{7,15},{8,0},{9,1},... | collective-permute-start | bytes 442376 | tf_op jit(solution)/shard_map/ppermute | solution.py:78
  90.1 0.0 collective-permute-done.22.refs_1_
  90.1 0.1 collective-permute-start.20
  90.2 0.4 collective-permute-start.21
  90.6 0.5 collective-permute-done.33.theirs_ref
  91.1 1.8 %collective-permute-start.15 = (bf16[512,1024]{1,0:T(8,128)(2,1)S(1)}, bf16[512,1024]{1,0:T(8,128)(2,1)S(1)}, u32[]{:S(2)}, u32[]{:S(2)}) collective-permute-start(bf16[512,1024]{1,0:T(8,128)(2,1)S(1)} %collective-permute-done.refs_0_), channel_id=1, source_target_pairs={{0,32},{1,33},{2,34},{3,35},{4,36},{5,37},{6,38},{7,39},{8,104},{9... | collective-permute-start | bytes 3145736 | tf_op jit(solution)/shard_map/ppermute | solution.py:78
  92.8 0.0 collective-permute-done.1.refs_0_
  92.8 3.0 %collective-permute-start.2 = (bf16[512,1024]{1,0:T(8,128)(2,1)S(1)}, bf16[512,1024]{1,0:T(8,128)(2,1)S(1)}, u32[]{:S(2)}, u32[]{:S(2)}) collective-permute-start(bf16[512,1024]{1,0:T(8,128)(2,1)S(1)} %collective-permute-done.1.refs_0_), channel_id=1, source_target_pairs={{0,1},{1,16},{2,3},{3,18},{4,5},{5,20},{6,7},{7,22},{8,25},{9,8},{... | collective-permute-start | bytes 3145736 | tf_op jit(solution)/shard_map/ppermute | solution.py:78
  95.8 1.2 collective-permute-start.4
  97.1 0.5 collective-permute-start.17
  97.6 8.7 %collective-permute-done.15.refs_2_ = bf16[512,1024]{1,0:T(8,128)(2,1)S(1)} collective-permute-done((bf16[512,1024]{1,0:T(8,128)(2,1)S(1)}, bf16[512,1024]{1,0:T(8,128)(2,1)S(1)}, u32[]{:S(2)}, u32[]{:S(2)}) %collective-permute-start.15) | collective-permute-done | bytes 1048608 | tf_op jit(solution)/shard_map/ppermute | solution.py:78
  106.2 0.0 collective-permute-start.18
  106.2 1.3 collective-permute-done.2.refs_0_
  107.6 0.2 collective-permute-start.5
  107.8 9.4 %collective-permute-done.4.refs_1_ = bf16[512,1024]{1,0:T(8,128)(2,1)S(1)} collective-permute-done((bf16[512,1024]{1,0:T(8,128)(2,1)S(1)}, bf16[512,1024]{1,0:T(8,128)(2,1)S(1)}, u32[]{:S(2)}, u32[]{:S(2)}) %collective-permute-start.4) | collective-permute-done | bytes 1048608 | tf_op jit(solution)/shard_map/ppermute | solution.py:78
  117.2 0.3 collective-permute-start.6
  117.5 2.3 %shard_map.94.refs_7_ = bf16[512,8192]{1,0:T(8,128)(2,1)} custom-call(bf16[512,1024]{1,0:T(8,128)(2,1)S(1)} %get-tuple-element.17.refs_0_, bf16[512,1024]{1,0:T(8,128)(2,1)S(1)} %collective-permute-done.22.refs_1_, bf16[512,1024]{1,0:T(8,128)(2,1)S(1)} %copy-done, bf16[512,64]{1,0:T(8,128)(2,1)S(1)} %get-tuple-element.19.refs_3_.refs_5_.refs_7_, ...), custom_call_target="tpu_custom_call" | custom-call | flops 1153433600 | bytes 4200000 | tf_op jit(solution)/shard_map/pallas_call | solution.py:359
  119.8 0.7 in_order.1
  120.6 4.4 %shard_map.95.refs_9_ = bf16[512,8192]{1,0:T(8,128)(2,1)} custom-call(bf16[512,1024]{1,0:T(8,128)(2,1)S(1)} %collective-permute-done.refs_0_, bf16[512,1024]{1,0:T(8,128)(2,1)S(1)} %collective-permute-done.19.refs_1_, bf16[512,1024]{1,0:T(8,128)(2,1)S(1)} %collective-permute-done.20.refs_2_, ...), custom_call_target="tpu_custom_call", output_to_operand_aliasing={{}: (7, {})} | custom-call | flops 2306867200 | bytes 7400000 | tf_op jit(solution)/shard_map/pallas_call | solution.py:359
  125.0 6.3 %shard_map.96.refs_7_ = bf16[512,8192]{1,0:T(8,128)(2,1)} custom-call(bf16[512,1024]{1,0:T(8,128)(2,1)S(1)} %collective-permute-done.1.refs_0_, bf16[512,1024]{1,0:T(8,128)(2,1)S(1)} %collective-permute-done.3.refs_1_, bf16[512,1024]{1,0:T(8,128)(2,1)S(1)} %collective-permute-done.15.refs_2_, ...), custom_call_target="tpu_custom_call", output_to_operand_aliasing={{}: (9, {})} | custom-call | flops 3460300800 | bytes 10600000 | tf_op jit(solution)/shard_map/pallas_call | solution.py:359
  131.3 4.4 %shard_map.97 = bf16[512,8192]{1,0:T(8,128)(2,1)} custom-call(bf16[512,1024]{1,0:T(8,128)(2,1)S(1)} %collective-permute-done.2.refs_0_, bf16[512,1024]{1,0:T(8,128)(2,1)S(1)} %collective-permute-done.4.refs_1_, bf16[512,1024]{1,0:T(8,128)(2,1)S(1)} %collective-permute-done.5.refs_2_, ...), custom_call_target="tpu_custom_call", output_to_operand_aliasing={{}: (7, {})} | custom-call | flops 2306867200 | bytes 7400000 | tf_op jit(solution)/shard_map/pallas_call | solution.py:359
  (25 shorter events, 0.2 us)
Async XLA Ops:
  0.6 0.9 copy-start.1
  1.5 0.7 copy-start.2
  2.3 25.0 %copy-start = (bf16[512,1024]{1,0:T(8,128)(2,1)S(1)}, bf16[512,1024]{1,0:T(8,128)(2,1)}, u32[]{:S(2)}) copy-start(bf16[512,1024]{1,0:T(8,128)(2,1)} %refs_4_.3) | copy-start | bytes 3145732
  2.3 4.8 %collective-permute-start.7 = (bf16[32,1152]{1,0:T(8,128)(2,1)S(1)}, bf16[32,1152]{1,0:T(8,128)(2,1)S(1)}, u32[]{:S(2)}, u32[]{:S(2)}) collective-permute-start(bf16[32,1152]{1,0:T(8,128)(2,1)S(1)} %pack.1.mine_ref), channel_id=1, source_target_pairs={{0,1},{1,16},{2,3},{3,18},{4,5},{5,20},{6,7},{7,22},{8,25},{9,8},{... | collective-permute-start | bytes 221192 | tf_op jit(solution)/shard_map/ppermute | solution.py:78
  7.1 7.7 %collective-permute-start.8 = (bf16[2,32,1152]{2,1,0:T(8,128)(2,1)S(1)}, bf16[2,32,1152]{2,1,0:T(8,128)(2,1)S(1)}, u32[]{:S(2)}, u32[]{:S(2)}) collective-permute-start(bf16[2,32,1152]{2,1,0:T(8,128)(2,1)S(1)} %join.1.refs_0_), channel_id=1, source_target_pairs={{0,6},{1,7},{2,0},{3,1},{4,2},{5,3},{6,4},{7,5},{8,14},{9,15},{10,... | collective-permute-start | bytes 442376 | tf_op jit(solution)/shard_map/ppermute | solution.py:78
  10.9 7.3 %collective-permute-start.9 = (bf16[2,32,1152]{2,1,0:T(8,128)(2,1)S(1)}, bf16[2,32,1152]{2,1,0:T(8,128)(2,1)S(1)}, u32[]{:S(2)}, u32[]{:S(2)}) collective-permute-start(bf16[2,32,1152]{2,1,0:T(8,128)(2,1)S(1)} %join.1.refs_0_), channel_id=1, source_target_pairs={{0,4},{1,5},{2,6},{3,7},{4,0},{5,1},{6,2},{7,3},{8,12},{9,13},{10,... | collective-permute-start | bytes 442376 | tf_op jit(solution)/shard_map/ppermute | solution.py:78
  10.9 9.5 %collective-permute-start.10 = (bf16[2,32,1152]{2,1,0:T(8,128)(2,1)S(1)}, bf16[2,32,1152]{2,1,0:T(8,128)(2,1)S(1)}, u32[]{:S(2)}, u32[]{:S(2)}) collective-permute-start(bf16[2,32,1152]{2,1,0:T(8,128)(2,1)S(1)} %join.1.refs_0_), channel_id=1, source_target_pairs={{0,2},{1,3},{2,4},{3,5},{4,6},{5,7},{6,0},{7,1},{8,10},{9,11},{10,... | collective-permute-start | bytes 442376 | tf_op jit(solution)/shard_map/ppermute | solution.py:78
  11.6 15.7 %collective-permute-start.11 = (bf16[2,32,1152]{2,1,0:T(8,128)(2,1)S(1)}, bf16[2,32,1152]{2,1,0:T(8,128)(2,1)S(1)}, u32[]{:S(2)}, u32[]{:S(2)}) collective-permute-start(bf16[2,32,1152]{2,1,0:T(8,128)(2,1)S(1)} %join.1.refs_0_), channel_id=1, source_target_pairs={{0,8},{1,9},{2,10},{3,11},{4,12},{5,13},{6,14},{7,15},{8,0},{9,1},... | collective-permute-start | bytes 442376 | tf_op jit(solution)/shard_map/ppermute | solution.py:78
  14.8 12.5 %collective-permute-start.12 = (bf16[2,32,1152]{2,1,0:T(8,128)(2,1)S(1)}, bf16[2,32,1152]{2,1,0:T(8,128)(2,1)S(1)}, u32[]{:S(2)}, u32[]{:S(2)}) collective-permute-start(bf16[2,32,1152]{2,1,0:T(8,128)(2,1)S(1)} %collective-permute-done.8.refs_1_), channel_id=1, source_target_pairs={{0,8},{1,9},{2,10},{3,11},{4,12},{5,13},{6,14},{7,15},{8,0},{9,1},... | collective-permute-start | bytes 442376 | tf_op jit(solution)/shard_map/ppermute | solution.py:78
  18.1 9.1 %collective-permute-start.13 = (bf16[2,32,1152]{2,1,0:T(8,128)(2,1)S(1)}, bf16[2,32,1152]{2,1,0:T(8,128)(2,1)S(1)}, u32[]{:S(2)}, u32[]{:S(2)}) collective-permute-start(bf16[2,32,1152]{2,1,0:T(8,128)(2,1)S(1)} %collective-permute-done.9.refs_2_), channel_id=1, source_target_pairs={{0,8},{1,9},{2,10},{3,11},{4,12},{5,13},{6,14},{7,15},{8,0},{9,1},... | collective-permute-start | bytes 442376 | tf_op jit(solution)/shard_map/ppermute | solution.py:78
  20.4 6.9 %collective-permute-start.14 = (bf16[2,32,1152]{2,1,0:T(8,128)(2,1)S(1)}, bf16[2,32,1152]{2,1,0:T(8,128)(2,1)S(1)}, u32[]{:S(2)}, u32[]{:S(2)}) collective-permute-start(bf16[2,32,1152]{2,1,0:T(8,128)(2,1)S(1)} %collective-permute-done.10.refs_3_), channel_id=1, source_target_pairs={{0,8},{1,9},{2,10},{3,11},{4,12},{5,13},{6,14},{7,15},{8,0},{9,1},... | collective-permute-start | bytes 442376 | tf_op jit(solution)/shard_map/ppermute | solution.py:78
  21.5 0.7 copy-start.3
  26.5 15.6 %collective-permute-start = (bf16[512,1024]{1,0:T(8,128)(2,1)S(1)}, bf16[512,1024]{1,0:T(8,128)(2,1)S(1)}, u32[]{:S(2)}, u32[]{:S(2)}) collective-permute-start(bf16[512,1024]{1,0:T(8,128)(2,1)S(1)} %get-tuple-element.17.refs_0_), channel_id=1, source_target_pairs={{0,2},{1,3},{2,4},{3,5},{4,6},{5,7},{6,0},{7,1},{8,14},{9,15},{10,... | collective-permute-start | bytes 3145736 | tf_op jit(solution)/shard_map/ppermute | solution.py:78
  32.2 3.6 %collective-permute-start.23 = (bf16[4,2,32,1152]{3,2,1,0:T(8,128)(2,1)S(1)}, bf16[4,2,32,1152]{3,2,1,0:T(8,128)(2,1)S(1)}, u32[]{:S(2)}, u32[]{:S(2)}) collective-permute-start(bf16[4,2,32,1152]{3,2,1,0:T(8,128)(2,1)S(1)} %get-tuple-element.22), channel_id=1, source_target_pairs={{0,8},{1,9},{2,10},{3,11},{4,12},{5,13},{6,14},{7,15},{8,0},{9,1},... | collective-permute-start | bytes 1769480 | tf_op jit(solution)/shard_map/ppermute | solution.py:78
  32.3 57.8 %collective-permute-start.22 = (bf16[512,1024]{1,0:T(8,128)(2,1)S(1)}, bf16[512,1024]{1,0:T(8,128)(2,1)S(1)}, u32[]{:S(2)}, u32[]{:S(2)}) collective-permute-start(bf16[512,1024]{1,0:T(8,128)(2,1)S(1)} %get-tuple-element.17.refs_0_), channel_id=1, source_target_pairs={{0,8},{1,9},{2,10},{3,11},{4,12},{5,13},{6,14},{7,15},{8,0},{9,1},... | collective-permute-start | bytes 3145736 | tf_op jit(solution)/shard_map/ppermute | solution.py:78
  32.8 57.4 %collective-permute-start.19 = (bf16[512,1024]{1,0:T(8,128)(2,1)S(1)}, bf16[512,1024]{1,0:T(8,128)(2,1)S(1)}, u32[]{:S(2)}, u32[]{:S(2)}) collective-permute-start(bf16[512,1024]{1,0:T(8,128)(2,1)S(1)} %get-tuple-element.17.refs_0_), channel_id=1, source_target_pairs={{0,1},{1,16},{2,3},{3,18},{4,5},{5,20},{6,7},{7,22},{8,25},{9,8},{... | collective-permute-start | bytes 3145736 | tf_op jit(solution)/shard_map/ppermute | solution.py:78
  35.9 7.1 %collective-permute-start.24 = (bf16[2,32,1152]{2,1,0:T(8,128)(2,1)S(1)}, bf16[2,32,1152]{2,1,0:T(8,128)(2,1)S(1)}, u32[]{:S(2)}, u32[]{:S(2)}) collective-permute-start(bf16[2,32,1152]{2,1,0:T(8,128)(2,1)S(1)} %get-tuple-element.24), channel_id=1, source_target_pairs={{0,2},{1,3},{2,4},{3,5},{4,6},{5,7},{6,0},{7,1},{8,10},{9,11},{10,... | collective-permute-start | bytes 442376 | tf_op jit(solution)/shard_map/ppermute | solution.py:78
  36.8 7.1 %collective-permute-start.25 = (bf16[2,32,1152]{2,1,0:T(8,128)(2,1)S(1)}, bf16[2,32,1152]{2,1,0:T(8,128)(2,1)S(1)}, u32[]{:S(2)}, u32[]{:S(2)}) collective-permute-start(bf16[2,32,1152]{2,1,0:T(8,128)(2,1)S(1)} %get-tuple-element.25), channel_id=1, source_target_pairs={{0,6},{1,7},{2,0},{3,1},{4,2},{5,3},{6,4},{7,5},{8,14},{9,15},{10,... | collective-permute-start | bytes 442376 | tf_op jit(solution)/shard_map/ppermute | solution.py:78
  42.1 5.5 %collective-permute-start.26 = (bf16[2,32,1152]{2,1,0:T(8,128)(2,1)S(1)}, bf16[2,32,1152]{2,1,0:T(8,128)(2,1)S(1)}, u32[]{:S(2)}, u32[]{:S(2)}) collective-permute-start(bf16[2,32,1152]{2,1,0:T(8,128)(2,1)S(1)} %get-tuple-element.26), channel_id=1, source_target_pairs={{0,4},{1,5},{2,6},{3,7},{4,0},{5,1},{6,2},{7,3},{8,12},{9,13},{10,... | collective-permute-start | bytes 442376 | tf_op jit(solution)/shard_map/ppermute | solution.py:78
  43.0 49.8 %collective-permute-start.1 = (bf16[512,1024]{1,0:T(8,128)(2,1)S(1)}, bf16[512,1024]{1,0:T(8,128)(2,1)S(1)}, u32[]{:S(2)}, u32[]{:S(2)}) collective-permute-start(bf16[512,1024]{1,0:T(8,128)(2,1)S(1)} %collective-permute-done.refs_0_), channel_id=1, source_target_pairs={{0,2},{1,3},{2,4},{3,5},{4,6},{5,7},{6,0},{7,1},{8,14},{9,15},{10,... | collective-permute-start | bytes 3145736 | tf_op jit(solution)/shard_map/ppermute | solution.py:78
  43.9 52.0 %collective-permute-start.3 = (bf16[512,1024]{1,0:T(8,128)(2,1)S(1)}, bf16[512,1024]{1,0:T(8,128)(2,1)S(1)}, u32[]{:S(2)}, u32[]{:S(2)}) collective-permute-start(bf16[512,1024]{1,0:T(8,128)(2,1)S(1)} %collective-permute-done.refs_0_), channel_id=1, source_target_pairs={{0,1},{1,16},{2,3},{3,18},{4,5},{5,20},{6,7},{7,22},{8,25},{9,8},{... | collective-permute-start | bytes 3145736 | tf_op jit(solution)/shard_map/ppermute | solution.py:78
  47.7 5.9 %collective-permute-start.27 = (bf16[32,1152]{1,0:T(8,128)(2,1)S(1)}, bf16[32,1152]{1,0:T(8,128)(2,1)S(1)}, u32[]{:S(2)}, u32[]{:S(2)}) collective-permute-start(bf16[32,1152]{1,0:T(8,128)(2,1)S(1)} %get-tuple-element.28), channel_id=1, source_target_pairs={{0,1},{1,16},{2,3},{3,18},{4,5},{5,20},{6,7},{7,22},{8,9},{9,24},{... | collective-permute-start | bytes 221192 | tf_op jit(solution)/shard_map/ppermute | solution.py:78
  53.6 5.9 %collective-permute-start.28 = (bf16[32,1152]{1,0:T(8,128)(2,1)S(1)}, bf16[32,1152]{1,0:T(8,128)(2,1)S(1)}, u32[]{:S(2)}, u32[]{:S(2)}) collective-permute-start(bf16[32,1152]{1,0:T(8,128)(2,1)S(1)} %get-tuple-element.28), channel_id=1, source_target_pairs={{0,17},{1,0},{2,19},{3,2},{4,21},{5,4},{6,23},{7,6},{8,25},{9,8},{... | collective-permute-start | bytes 221192 | tf_op jit(solution)/shard_map/ppermute | solution.py:78
  59.5 5.5 %collective-permute-start.29 = (bf16[32,1152]{1,0:T(8,128)(2,1)S(1)}, bf16[32,1152]{1,0:T(8,128)(2,1)S(1)}, u32[]{:S(2)}, u32[]{:S(2)}) collective-permute-start(bf16[32,1152]{1,0:T(8,128)(2,1)S(1)} %get-tuple-element.27.refs_0_), channel_id=1, source_target_pairs={{0,16},{1,17},{2,18},{3,19},{4,20},{5,21},{6,22},{7,23},{8,24},{9,... | collective-permute-start | bytes 221192 | tf_op jit(solution)/shard_map/ppermute | solution.py:78
  65.0 4.5 %collective-permute-start.30 = (bf16[32,1152]{1,0:T(8,128)(2,1)S(1)}, bf16[32,1152]{1,0:T(8,128)(2,1)S(1)}, u32[]{:S(2)}, u32[]{:S(2)}) collective-permute-start(bf16[32,1152]{1,0:T(8,128)(2,1)S(1)} %shard_map.99.refs_0_), channel_id=1, source_target_pairs={{0,32},{1,33},{2,34},{3,35},{4,36},{5,37},{6,38},{7,39},{8,40},{9,... | collective-permute-start | bytes 221192 | tf_op jit(solution)/shard_map/ppermute | solution.py:78
  69.5 3.5 %collective-permute-start.31 = (bf16[32,1152]{1,0:T(8,128)(2,1)S(1)}, bf16[32,1152]{1,0:T(8,128)(2,1)S(1)}, u32[]{:S(2)}, u32[]{:S(2)}) collective-permute-start(bf16[32,1152]{1,0:T(8,128)(2,1)S(1)} %shard_map.99.refs_0_), channel_id=1, source_target_pairs={{0,96},{1,97},{2,98},{3,99},{4,100},{5,101},{6,102},{7,103},{8,104... | collective-permute-start | bytes 221192 | tf_op jit(solution)/shard_map/ppermute | solution.py:78
  73.0 4.7 %collective-permute-start.32 = (bf16[32,1152]{1,0:T(8,128)(2,1)S(1)}, bf16[32,1152]{1,0:T(8,128)(2,1)S(1)}, u32[]{:S(2)}, u32[]{:S(2)}) collective-permute-start(bf16[32,1152]{1,0:T(8,128)(2,1)S(1)} %shard_map.99.refs_0_), channel_id=1, source_target_pairs={{0,64},{1,65},{2,66},{3,67},{4,68},{5,69},{6,70},{7,71},{8,72},{9,... | collective-permute-start | bytes 221192 | tf_op jit(solution)/shard_map/ppermute | solution.py:78
  77.8 13.3 %collective-permute-start.33 = (f32[32,1152]{1,0:T(8,128)S(1)}, f32[32,1152]{1,0:T(8,128)S(1)}, u32[]{:S(2)}, u32[]{:S(2)}) collective-permute-start(f32[32,1152]{1,0:T(8,128)S(1)} %shard_map.100.mine_ref), channel_id=1, source_target_pairs={{0,8},{1,9},{2,10},{3,11},{4,12},{5,13},{6,14},{7,15},{8,0},{9,1},... | collective-permute-start | bytes 442376 | tf_op jit(solution)/shard_map/ppermute | solution.py:78
  90.1 7.0 %collective-permute-start.20 = (bf16[512,1024]{1,0:T(8,128)(2,1)S(1)}, bf16[512,1024]{1,0:T(8,128)(2,1)S(1)}, u32[]{:S(2)}, u32[]{:S(2)}) collective-permute-start(bf16[512,1024]{1,0:T(8,128)(2,1)S(1)} %collective-permute-done.refs_0_), channel_id=1, source_target_pairs={{0,8},{1,9},{2,10},{3,11},{4,12},{5,13},{6,14},{7,15},{8,0},{9,1},... | collective-permute-start | bytes 3145736 | tf_op jit(solution)/shard_map/ppermute | solution.py:78
  90.2 6.9 %collective-permute-start.21 = (bf16[512,1024]{1,0:T(8,128)(2,1)S(1)}, bf16[512,1024]{1,0:T(8,128)(2,1)S(1)}, u32[]{:S(2)}, u32[]{:S(2)}) collective-permute-start(bf16[512,1024]{1,0:T(8,128)(2,1)S(1)} %collective-permute-done.19.refs_1_), channel_id=1, source_target_pairs={{0,8},{1,9},{2,10},{3,11},{4,12},{5,13},{6,14},{7,15},{8,0},{9,1},... | collective-permute-start | bytes 3145736 | tf_op jit(solution)/shard_map/ppermute | solution.py:78
  91.1 15.2 %collective-permute-start.15 = (bf16[512,1024]{1,0:T(8,128)(2,1)S(1)}, bf16[512,1024]{1,0:T(8,128)(2,1)S(1)}, u32[]{:S(2)}, u32[]{:S(2)}) collective-permute-start(bf16[512,1024]{1,0:T(8,128)(2,1)S(1)} %collective-permute-done.refs_0_), channel_id=1, source_target_pairs={{0,32},{1,33},{2,34},{3,35},{4,36},{5,37},{6,38},{7,39},{8,104},{9... | collective-permute-start | bytes 3145736 | tf_op jit(solution)/shard_map/ppermute | solution.py:78
  92.8 14.8 %collective-permute-start.2 = (bf16[512,1024]{1,0:T(8,128)(2,1)S(1)}, bf16[512,1024]{1,0:T(8,128)(2,1)S(1)}, u32[]{:S(2)}, u32[]{:S(2)}) collective-permute-start(bf16[512,1024]{1,0:T(8,128)(2,1)S(1)} %collective-permute-done.1.refs_0_), channel_id=1, source_target_pairs={{0,1},{1,16},{2,3},{3,18},{4,5},{5,20},{6,7},{7,22},{8,25},{9,8},{... | collective-permute-start | bytes 3145736 | tf_op jit(solution)/shard_map/ppermute | solution.py:78
  95.8 21.3 %collective-permute-start.4 = (bf16[512,1024]{1,0:T(8,128)(2,1)S(1)}, bf16[512,1024]{1,0:T(8,128)(2,1)S(1)}, u32[]{:S(2)}, u32[]{:S(2)}) collective-permute-start(bf16[512,1024]{1,0:T(8,128)(2,1)S(1)} %collective-permute-done.3.refs_1_), channel_id=1, source_target_pairs={{0,32},{1,33},{2,34},{3,35},{4,36},{5,37},{6,38},{7,39},{8,104},{9... | collective-permute-start | bytes 3145736 | tf_op jit(solution)/shard_map/ppermute | solution.py:78
  97.1 27.9 %collective-permute-start.16 = (bf16[512,1024]{1,0:T(8,128)(2,1)S(1)}, bf16[512,1024]{1,0:T(8,128)(2,1)S(1)}, u32[]{:S(2)}, u32[]{:S(2)}) collective-permute-start(bf16[512,1024]{1,0:T(8,128)(2,1)S(1)} %collective-permute-done.1.refs_0_), channel_id=1, source_target_pairs={{0,8},{1,9},{2,10},{3,11},{4,12},{5,13},{6,14},{7,15},{8,0},{9,1},... | collective-permute-start | bytes 3145736 | tf_op jit(solution)/shard_map/ppermute | solution.py:78
  97.1 27.9 %collective-permute-start.17 = (bf16[512,1024]{1,0:T(8,128)(2,1)S(1)}, bf16[512,1024]{1,0:T(8,128)(2,1)S(1)}, u32[]{:S(2)}, u32[]{:S(2)}) collective-permute-start(bf16[512,1024]{1,0:T(8,128)(2,1)S(1)} %collective-permute-done.3.refs_1_), channel_id=1, source_target_pairs={{0,8},{1,9},{2,10},{3,11},{4,12},{5,13},{6,14},{7,15},{8,0},{9,1},... | collective-permute-start | bytes 3145736 | tf_op jit(solution)/shard_map/ppermute | solution.py:78
  106.2 18.8 %collective-permute-start.18 = (bf16[512,1024]{1,0:T(8,128)(2,1)S(1)}, bf16[512,1024]{1,0:T(8,128)(2,1)S(1)}, u32[]{:S(2)}, u32[]{:S(2)}) collective-permute-start(bf16[512,1024]{1,0:T(8,128)(2,1)S(1)} %collective-permute-done.15.refs_2_), channel_id=1, source_target_pairs={{0,8},{1,9},{2,10},{3,11},{4,12},{5,13},{6,14},{7,15},{8,0},{9,1},... | collective-permute-start | bytes 3145736 | tf_op jit(solution)/shard_map/ppermute | solution.py:78
  107.6 23.7 %collective-permute-start.5 = (bf16[512,1024]{1,0:T(8,128)(2,1)S(1)}, bf16[512,1024]{1,0:T(8,128)(2,1)S(1)}, u32[]{:S(2)}, u32[]{:S(2)}) collective-permute-start(bf16[512,1024]{1,0:T(8,128)(2,1)S(1)} %collective-permute-done.2.refs_0_), channel_id=1, source_target_pairs={{0,8},{1,9},{2,10},{3,11},{4,12},{5,13},{6,14},{7,15},{8,0},{9,1},... | collective-permute-start | bytes 3145736 | tf_op jit(solution)/shard_map/ppermute | solution.py:78
  117.2 14.1 %collective-permute-start.6 = (bf16[512,1024]{1,0:T(8,128)(2,1)S(1)}, bf16[512,1024]{1,0:T(8,128)(2,1)S(1)}, u32[]{:S(2)}, u32[]{:S(2)}) collective-permute-start(bf16[512,1024]{1,0:T(8,128)(2,1)S(1)} %collective-permute-done.4.refs_1_), channel_id=1, source_target_pairs={{0,8},{1,9},{2,10},{3,11},{4,12},{5,13},{6,14},{7,15},{8,0},{9,1},... | collective-permute-start | bytes 3145736 | tf_op jit(solution)/shard_map/ppermute | solution.py:78

commit v2 on v1

--- a/solution.py
+++ b/solution.py
@@ -59,6 +59,11 @@
     return x, y, (z + step) % 4, core
 
 
+def z_back(x, y, z, core):
+    step = 1 if (core + y) % 2 == 0 else -1
+    return x, y, (z - step) % 4, core
+
+
 def x_hop(x, y, z, core):
     step = 1 if core == 0 else -1
     return (x + step) % 4, y, z, core
@@ -90,36 +95,50 @@
     return y, core, z, xl
 
 
+def z_offsets():
+    y, core, _, _ = position()
+    odd = lax.rem(core + y, 2)
+    return 0, 3 - 2 * odd, 1 + 2 * odd, 2
+
+
+PLACES = ((0, 0), (1, 0), (0, 1), (3, 0), (1, 1), (2, 0), (3, 1), (2, 1))
+MIRROR = (0, 2, 1, 3)
+
+
 def piece_place(slot):
-    y, core, _, _ = position()
-    half = core if slot < 8 else 1 - core
-    step = 1 - 2 * lax.rem(half + y, 2)
-    ups = (0, -step, 0, 2, -step, step, 2, step)
-    crosses = (0, 0, 1, 0, 1, 0, 1, 1)
-    return lax.rem(ups[slot % 8] + 4, 4), crosses[slot % 8], half
-
-
-def shard_at(up, cross):
+    _, core, _, _ = position()
+    place, cross = PLACES[slot % 8]
+    return (place, cross, core) if slot < 8 else (MIRROR[place], cross, 1 - core)
+
+
+def shard_at(place, cross):
     _, _, z, xl = position()
-    return lax.rem(z + up, 4) * 2 + lax.rem(xl + cross, 2)
-
-
-def pack_kernel(down_ref, up_ref, packed_ref):
+    return lax.rem(z + z_offsets()[place], 4) * 2 + lax.rem(xl + cross, 2)
+
+
+def pack_kernel(down_ref, up_ref, packed_ref, arrived):
     _, core, _, _ = position()
     ranks = pl.ds(pl.multiple_of(core * RANK_HALF, RANK_HALF), RANK_HALF)
-    packed_ref[:, :SHARD] = down_ref[ranks, :]
-    packed_ref[:, SHARD:] = up_ref[ranks, :]
+    copies = [
+        pltpu.make_async_copy(down_ref.at[ranks], packed_ref.at[:, :SHARD], arrived.at[0]),
+        pltpu.make_async_copy(up_ref.at[ranks], packed_ref.at[:, SHARD:], arrived.at[1]),
+    ]
+    for copy in copies:
+        copy.start()
+    for copy in copies:
+        copy.wait()
 
 
 def packed_half(down_adapter, up_adapter):
     return pl.pallas_call(
         pack_kernel,
-        in_specs=[VMEM, VMEM],
+        in_specs=[HBM, HBM],
         out_specs=VMEM,
         out_shape=pltpu.VMEM((RANK_HALF, PACKED), jnp.bfloat16),
+        scratch_shapes=[pltpu.SemaphoreType.DMA((2,))],
         compiler_params=LIMIT,
         name="pack",
-    )(down_adapter, up_adapter)
+    )(in_hbm(down_adapter), in_hbm(up_adapter))
 
 
 def join_kernel(mine_ref, crossed_ref, pair_ref):
@@ -140,7 +159,7 @@
 
 def prepare_kernel(
     codes_ref, scale_ref, col_ref, acts_ref,
-    weight_ref, held_ref, words_ref, scales_ref, rows_ref, arrived
+    weight_ref, held_ref, words_ref, scales_ref, columns_ref, rows_ref, arrived
 ):
     _, core, _, _ = position()
     first = pl.multiple_of(core * 8, 8)
@@ -151,7 +170,9 @@
         )
         for i in range(4)
     ]
+    columns = pltpu.make_async_copy(col_ref, columns_ref, arrived.at[13])
     scales.start()
+    columns.start()
     for copy in words:
         copy.start()
     acts = [
@@ -161,12 +182,13 @@
         for i in range(8)
     ]
     scales.wait()
+    columns.wait()
     for copy in acts:
         copy.start()
 
     def block(b):
         absmax = scales_ref[pl.ds(b, 1), :].astype(jnp.float32)
-        absmax = (absmax + 1.0) / 256.0 * col_ref[...]
+        absmax = (absmax + 1.0) / 256.0 * columns_ref[...]
         for lane in range(COLS // 128):
             code = words_ref[b, :, lane * 128 : (lane + 1) * 128]
             scale = absmax[:, lane * 128 : (lane + 1) * 128]
@@ -194,7 +216,7 @@
 def prepared(codes, scale_codes, col_scale, acts):
     return pl.pallas_call(
         prepare_kernel,
-        in_specs=[HBM, HBM, VMEM, HBM],
+        in_specs=[HBM, HBM, HBM, HBM],
         out_specs=[VMEM, VMEM],
         out_shape=[
             pltpu.VMEM((HALF, COLS), jnp.bfloat16),
@@ -203,15 +225,16 @@
         scratch_shapes=[
             pltpu.VMEM((8, 16, COLS), jnp.int32),
             pltpu.VMEM((8, COLS), jnp.int32),
+            pltpu.VMEM((1, COLS), jnp.float32),
             pltpu.VMEM((COLS // 128, 64, 128), jnp.float32),
-            pltpu.SemaphoreType.DMA((13,)),
+            pltpu.SemaphoreType.DMA((14,)),
         ],
         compiler_params=LIMIT,
         cost_estimate=pl.CostEstimate(
             flops=2_000_000_000, bytes_accessed=9_600_000, transcendentals=0
         ),
         name="prepare",
-    )(in_hbm(codes), in_hbm(scale_codes), col_scale.reshape(1, COLS), in_hbm(acts))
+    )(in_hbm(codes), in_hbm(scale_codes), in_hbm(col_scale.reshape(1, COLS)), in_hbm(acts))
 
 
 def in_hbm(value):
@@ -254,14 +277,14 @@
             acts, down_ref[up, cross], NT, preferred_element_type=jnp.float32
         )
         sums_ref[up, cross, :, :SHARD] = term[:RANK_HALF].astype(jnp.bfloat16)
-        rest_ref[up, cross, :, :SHARD] = term[RANK_HALF:].astype(jnp.bfloat16)
+        rest_ref[MIRROR[up], cross, :, :SHARD] = term[RANK_HALF:].astype(jnp.bfloat16)
     lowered = lowered.astype(jnp.bfloat16)
     for up, cross in order:
         term = lax.dot_general(
             lowered, grad_ref[:, columns(up, cross, UP)], TN, preferred_element_type=jnp.float32
         ).astype(jnp.bfloat16)
         sums_ref[up, cross, :, SHARD:] = term[:RANK_HALF]
-        rest_ref[up, cross, :, SHARD:] = term[RANK_HALF:]
+        rest_ref[MIRROR[up], cross, :, SHARD:] = term[RANK_HALF:]
 
 
 def adapter_terms(grad_out, own, other, acts):
@@ -303,8 +326,8 @@
     )(in_vmem(mine), in_vmem(arrived))
 
 
-def four_sums_kernel(split, scale, *refs):
-    ins, outs = refs[:4], refs[4:]
+def sums_kernel(split, scale, count, *refs):
+    ins, outs = refs[:count], refs[count:]
     total = ins[0][...].astype(jnp.float32)
     for ref in ins[1:]:
         total += ref[...].astype(jnp.float32)
@@ -314,11 +337,11 @@
         ref[...] = (total[i] if split else total).astype(ref.dtype)
 
 
-def four_sums(parts, split, dtype, scale=None):
-    shape = pltpu.VMEM((RANK_HALF, PACKED), dtype)
-    return pl.pallas_call(
-        functools.partial(four_sums_kernel, split, scale),
-        in_specs=[VMEM] * 4,
+def sums_of(parts, dtype, split=False, scale=None):
+    shape = pltpu.VMEM(parts[0].shape[1:] if split else parts[0].shape, dtype)
+    return pl.pallas_call(
+        functools.partial(sums_kernel, split, scale, len(parts)),
+        in_specs=[VMEM] * len(parts),
         out_specs=[VMEM] * 2 if split else VMEM,
         out_shape=[shape] * 2 if split else shape,
         compiler_params=LIMIT,
@@ -411,11 +434,13 @@
     crossed = moved(packed, x_hop)
     w, acts = prepared(codes, scale_codes, col_scale, acts)
     pair = joined(packed, crossed)
-    own, other = [pair] + [None] * 3, [None] * 4
-    for dz in (1, 3, 2):
-        own[4 - dz] = moved(pair, shifted("z", dz))
-    for up in (0, 3, 1, 2):
-        other[up] = moved(own[up], core_swap)
+    ahead = moved(pair, z_back)
+    behind = moved(pair, z_hop)
+    far = moved(ahead, z_back)
+    own = (pair, behind, ahead, far)
+    other = [None] * 4
+    for place in range(4):
+        other[MIRROR[place]] = moved(own[place], core_swap)
     w_z1 = moved(w, z_hop)
     w_x0 = moved(w, x_hop)
     w_z2 = moved(w_z1, z_hop)
@@ -427,28 +452,30 @@
     mixed, down, sums, rest = adapter_terms(grad_out, own, other, acts)
     arrived = moved(rest, core_swap)
     sums = core_sums(sums, arrived)
-    parts = [sums[0]]
-    for dz in (1, 3, 2):
-        parts.append(moved(sums[dz], shifted("z", dz)))
-    mine, cross = four_sums(parts, True, jnp.bfloat16)
+    relayed = moved(sums[3], z_back)
+    behind = moved(sums[2], z_hop)
+    relayed = sums_of((sums[1], relayed), jnp.bfloat16)
+    ahead = moved(relayed, z_back)
+    mine, cross = sums_of((sums[0], behind, ahead), jnp.bfloat16, split=True)
     parts = [mine]
-    for dx, part in ((1, cross), (3, cross), (2, mine)):
-        parts.append(moved(part, shifted("x", dx)))
-    mine = four_sums(parts, False, jnp.bfloat16)
+    for by, part in ((1, cross), (3, cross), (2, mine)):
+        parts.append(moved(part, shifted("x", by)))
+    mine = sums_of(parts, jnp.bfloat16)
     parts = [mine]
-    for dy in (1, 3, 2):
-        parts.append(moved(mine, shifted("y", dy)))
+    for by in (1, 3, 2):
+        parts.append(moved(mine, shifted("y", by)))
     scale = adapter_scale * float(TOKENS * DEVICES) ** (-0.5)
-    mine = four_sums(parts, False, jnp.float32, scale)
+    mine = sums_of(parts, jnp.float32, scale=scale)
 
     pieces = (w, w_z1, w_x0, w_z2, w_x1, w_y1, w_x2, w_xy)
     mirrored = []
     for piece in pieces:
         mirrored.append(moved(piece, core_swap))
     out = None
-    for stage in ((0,), (1, 2), (3, 4, 5), (6, 7)):
-        slots = stage + tuple(8 + k for k in stage)
-        weights = [pieces[k] for k in stage] + [mirrored[k] for k in stage]
+    turns = ((0, 8), (1, 2, 9, 10), (3, 4, 5, 11, 12, 13), (6, 7), (14, 15))
+    everything = (*pieces, *mirrored)
+    for slots in turns:
+        weights = [everything[k] for k in slots]
         out = product(slots, weights, grad_out, mixed, down, out)
 
     theirs = moved(mine, core_swap)

time: 136 us -> 137 us (level)
  waiting for transfers between devices: 48.4 us -> 54.4 us
  starting transfers between devices: 56.6 us -> 52.5 us
  local copies, waits for them, and re-layouts: 2.3 us -> 0.01 us
    ppermute x34, waiting for transfers between devices: 48.4 us -> 54.4 us  [moved(): return lax.ppermute(value, AXES, pairs)]
    ppermute x34, starting transfers between devices: 56.6 us -> 52.5 us  [moved(): return lax.ppermute(value, AXES, pairs)]
    unnamed x8 -> x2, local copies, waits for them, and re-layouts: 2.3 us -> 0.01 us
    pallas_call x5 -> x6, Pallas kernels: 4.49 us -> 5.47 us  [the longest x1 4.33 us: prepared(): pl.pallas_call(prepare_kernel, in_specs=[HBM, HBM, HBM, HBM], out_specs=[...]
    pallas_call x4 -> x5, Pallas kernels: 17.5 us -> 17.8 us  [product(): pl.pallas_call(functools.partial(product_kernel, slots, aliased), in_spec...]
  transfers between devices with their start and end apart: 34 -> 34, of which waited for: 14 -> 14; matrix products, arithmetic and copies ran while one was open for 0% -> 0% of each run, Pallas kernels for 17% -> 19%
where the time goes in v2:
time: 137 us
  waiting for transfers between devices  54.4 us (40%)
  starting transfers between devices  52.5 us (38%)
  Pallas kernels  29 us (21%)
    ppermute x34, waiting for transfers between devices, moved(): return lax.ppermute(value, AXES, pairs)  54.4 us
    ppermute x34, starting transfers between devices, moved(): return lax.ppermute(value, AXES, pairs)  52.5 us
    pallas_call x5, Pallas kernels, product(): pl.pallas_call(functools.partial(product_kernel, slots, aliased), in_spec...  17.8 us
    pallas_call x1, Pallas kernels, adapter_terms(): pl.pallas_call(adapter_kernel, in_specs=[VMEM] * 10, out_specs=[VMEM] * 4...  4.89 us
    pallas_call x1, Pallas kernels, prepared(): pl.pallas_call(prepare_kernel, in_specs=[HBM, HBM, HBM, HBM], out_specs=[...  4.33 us
  transfers between devices with their start and end apart: 34, of which 14 were waited for; matrix products, arithmetic and copies ran while one was open for 0% of the time, Pallas kernels for 19%

profile of v2, /device:TPU:1, one launch (start us, length us, event | category | flops | bytes accessed | tf_op | source)
XLA Modules:
  0.0 137.0 jit_solution(5263664316924753065)
XLA Ops:
  0.6 1.0 pack.1.mine_ref
  1.6 3.4 %collective-permute-start.7 = (bf16[32,1152]{1,0:T(8,128)(2,1)S(1)}, bf16[32,1152]{1,0:T(8,128)(2,1)S(1)}, u32[]{:S(2)}, u32[]{:S(2)}) collective-permute-start(bf16[32,1152]{1,0:T(8,128)(2,1)S(1)} %pack.1.mine_ref), channel_id=1, source_target_pairs={{0,1},{1,16},{2,3},{3,18},{4,5},{5,20},{6,7},{7,22},{8,25},{9,8},{... | collective-permute-start | bytes 221192 | tf_op jit(solution)/shard_map/ppermute | solution.py:83
  5.0 1.4 %collective-permute-done.7.crossed_ref = bf16[32,1152]{1,0:T(8,128)(2,1)S(1)} collective-permute-done((bf16[32,1152]{1,0:T(8,128)(2,1)S(1)}, bf16[32,1152]{1,0:T(8,128)(2,1)S(1)}, u32[]{:S(2)}, u32[]{:S(2)}) %collective-permute-start.7) | collective-permute-done | bytes 73760 | tf_op jit(solution)/shard_map/ppermute | solution.py:83
  6.4 1.7 %collective-permute-start.9 = (bf16[2,32,1152]{2,1,0:T(8,128)(2,1)S(1)}, bf16[2,32,1152]{2,1,0:T(8,128)(2,1)S(1)}, u32[]{:S(2)}, u32[]{:S(2)}) collective-permute-start(bf16[2,32,1152]{2,1,0:T(8,128)(2,1)S(1)} %join.1.refs_0_), channel_id=1, source_target_pairs={{0,6},{1,7},{2,0},{3,1},{4,2},{5,3},{6,4},{7,5},{8,10},{9,11},{10,... | collective-permute-start | bytes 442376 | tf_op jit(solution)/shard_map/ppermute | solution.py:83
  8.1 2.2 %collective-permute-start.8 = (bf16[2,32,1152]{2,1,0:T(8,128)(2,1)S(1)}, bf16[2,32,1152]{2,1,0:T(8,128)(2,1)S(1)}, u32[]{:S(2)}, u32[]{:S(2)}) collective-permute-start(bf16[2,32,1152]{2,1,0:T(8,128)(2,1)S(1)} %join.1.refs_0_), channel_id=1, source_target_pairs={{0,2},{1,3},{2,4},{3,5},{4,6},{5,7},{6,0},{7,1},{8,14},{9,15},{10,... | collective-permute-start | bytes 442376 | tf_op jit(solution)/shard_map/ppermute | solution.py:83
  10.3 2.5 %collective-permute-done.9.refs_2_ = bf16[2,32,1152]{2,1,0:T(8,128)(2,1)S(1)} collective-permute-done((bf16[2,32,1152]{2,1,0:T(8,128)(2,1)S(1)}, bf16[2,32,1152]{2,1,0:T(8,128)(2,1)S(1)}, u32[]{:S(2)}, u32[]{:S(2)}) %collective-permute-start.9) | collective-permute-done | bytes 147488 | tf_op jit(solution)/shard_map/ppermute | solution.py:83
  12.8 6.4 %collective-permute-start.11 = (bf16[2,32,1152]{2,1,0:T(8,128)(2,1)S(1)}, bf16[2,32,1152]{2,1,0:T(8,128)(2,1)S(1)}, u32[]{:S(2)}, u32[]{:S(2)}) collective-permute-start(bf16[2,32,1152]{2,1,0:T(8,128)(2,1)S(1)} %join.1.refs_0_), channel_id=1, source_target_pairs={{0,8},{1,9},{2,10},{3,11},{4,12},{5,13},{6,14},{7,15},{8,0},{9,1},... | collective-permute-start | bytes 442376 | tf_op jit(solution)/shard_map/ppermute | solution.py:83
  19.2 0.0 collective-permute-start.12
  19.2 0.0 collective-permute-done.8.refs_1_
  19.2 1.0 collective-permute-start.13
  20.2 1.7 %collective-permute-start.14 = (bf16[2,32,1152]{2,1,0:T(8,128)(2,1)S(1)}, bf16[2,32,1152]{2,1,0:T(8,128)(2,1)S(1)}, u32[]{:S(2)}, u32[]{:S(2)}) collective-permute-start(bf16[2,32,1152]{2,1,0:T(8,128)(2,1)S(1)} %collective-permute-done.10.refs_3_), channel_id=1, source_target_pairs={{0,8},{1,9},{2,10},{3,11},{4,12},{5,13},{6,14},{7,15},{8,0},{9,1},... | collective-permute-start | bytes 442376 | tf_op jit(solution)/shard_map/ppermute | solution.py:83
  21.9 4.3 %prepare.1 = (bf16[512,1024]{1,0:T(8,128)(2,1)S(1)}, bf16[512,8192]{1,0:T(8,128)(2,1)S(1)}) custom-call(s32[16,16,1024]{2,1,0:T(8,128)} %codes_ref.1, s32[16,1024]{1,0:T(8,128)} %scale_ref.1, f32[1,1024]{1,0:T(1,128)} %bitcast.1, bf16[512,8192]{1,0:T(8,128)(2,1)} %acts_ref.1), custom_call_target="tpu_custom_call" | custom-call | flops 2000000000 | bytes 9600000 | tf_op jit(solution)/shard_map/prepare/pallas_call | solution.py:217
  26.2 3.5 %collective-permute-start = (bf16[512,1024]{1,0:T(8,128)(2,1)S(1)}, bf16[512,1024]{1,0:T(8,128)(2,1)S(1)}, u32[]{:S(2)}, u32[]{:S(2)}) collective-permute-start(bf16[512,1024]{1,0:T(8,128)(2,1)S(1)} %get-tuple-element.17.refs_0_), channel_id=1, source_target_pairs={{0,2},{1,3},{2,4},{3,5},{4,6},{5,7},{6,0},{7,1},{8,14},{9,15},{10,... | collective-permute-start | bytes 3145736 | tf_op jit(solution)/shard_map/ppermute | solution.py:83
  29.7 0.0 collective-permute-done.11.refs_4_
  29.7 0.0 collective-permute-done.14.refs_7_
  29.7 4.9 %adapter.1 = (bf16[512,64]{1,0:T(8,128)(2,1)S(1)}, bf16[4,2,64,1024]{3,2,1,0:T(8,128)(2,1)S(1)}, bf16[4,2,32,1152]{3,2,1,0:T(8,128)(2,1)S(1)}, bf16[4,2,32,1152]{3,2,1,0:T(8,128)(2,1)S(1)}) custom-call(bf16[512,1024]{1,0:T(8,128)(2,1)S(1)} %copy-done, bf16[2,32,1152]{2,1,0:T(8,128)(2,1)S(1)} %join.1.refs_0_, ...), custom_call_target="tpu_custom_call" | custom-call | flops 5000000000 | bytes 12000000 | tf_op jit(solution)/shard_map/adapter/pallas_call | solution.py:292
  34.6 0.1 collective-permute-start.23
  34.7 0.5 collective-permute-start.22
  35.2 1.9 %collective-permute-start.19 = (bf16[512,1024]{1,0:T(8,128)(2,1)S(1)}, bf16[512,1024]{1,0:T(8,128)(2,1)S(1)}, u32[]{:S(2)}, u32[]{:S(2)}) collective-permute-start(bf16[512,1024]{1,0:T(8,128)(2,1)S(1)} %get-tuple-element.17.refs_0_), channel_id=1, source_target_pairs={{0,1},{1,16},{2,3},{3,18},{4,5},{5,20},{6,7},{7,22},{8,25},{9,8},{... | collective-permute-start | bytes 3145736 | tf_op jit(solution)/shard_map/ppermute | solution.py:83
  37.1 0.0 collective-permute-done.23.arrived_ref
  37.1 0.1 core_sums.1
  37.2 0.1 collective-permute-start.25
  37.3 2.7 %collective-permute-start.24 = (bf16[2,32,1152]{2,1,0:T(8,128)(2,1)S(1)}, bf16[2,32,1152]{2,1,0:T(8,128)(2,1)S(1)}, u32[]{:S(2)}, u32[]{:S(2)}) collective-permute-start(bf16[2,32,1152]{2,1,0:T(8,128)(2,1)S(1)} %get-tuple-element.24), channel_id=1, source_target_pairs={{0,2},{1,3},{2,4},{3,5},{4,6},{5,7},{6,0},{7,1},{8,14},{9,15},{10,... | collective-permute-start | bytes 442376 | tf_op jit(solution)/shard_map/ppermute | solution.py:83
  40.0 4.4 %collective-permute-done.25.refs_1_ = bf16[2,32,1152]{2,1,0:T(8,128)(2,1)S(1)} collective-permute-done((bf16[2,32,1152]{2,1,0:T(8,128)(2,1)S(1)}, bf16[2,32,1152]{2,1,0:T(8,128)(2,1)S(1)}, u32[]{:S(2)}, u32[]{:S(2)}) %collective-permute-start.25) | collective-permute-done | bytes 147488 | tf_op jit(solution)/shard_map/ppermute | solution.py:83
  44.4 0.1 collective-permute-start.26
  44.5 2.7 %collective-permute-start.1 = (bf16[512,1024]{1,0:T(8,128)(2,1)S(1)}, bf16[512,1024]{1,0:T(8,128)(2,1)S(1)}, u32[]{:S(2)}, u32[]{:S(2)}) collective-permute-start(bf16[512,1024]{1,0:T(8,128)(2,1)S(1)} %collective-permute-done.refs_0_), channel_id=1, source_target_pairs={{0,2},{1,3},{2,4},{3,5},{4,6},{5,7},{6,0},{7,1},{8,14},{9,15},{10,... | collective-permute-start | bytes 3145736 | tf_op jit(solution)/shard_map/ppermute | solution.py:83
  47.2 0.0 collective-permute-done.24.refs_1_
  47.2 1.5 %collective-permute-start.4 = (bf16[512,1024]{1,0:T(8,128)(2,1)S(1)}, bf16[512,1024]{1,0:T(8,128)(2,1)S(1)}, u32[]{:S(2)}, u32[]{:S(2)}) collective-permute-start(bf16[512,1024]{1,0:T(8,128)(2,1)S(1)} %collective-permute-done.refs_0_), channel_id=1, source_target_pairs={{0,1},{1,16},{2,3},{3,18},{4,5},{5,20},{6,7},{7,22},{8,25},{9,8},{... | collective-permute-start | bytes 3145736 | tf_op jit(solution)/shard_map/ppermute | solution.py:83
  48.6 1.5 %collective-permute-done.26.refs_2_ = bf16[2,32,1152]{2,1,0:T(8,128)(2,1)S(1)} collective-permute-done((bf16[2,32,1152]{2,1,0:T(8,128)(2,1)S(1)}, bf16[2,32,1152]{2,1,0:T(8,128)(2,1)S(1)}, u32[]{:S(2)}, u32[]{:S(2)}) %collective-permute-start.26) | collective-permute-done | bytes 147488 | tf_op jit(solution)/shard_map/ppermute | solution.py:83
  50.1 0.1 shard_map.100
  50.2 0.1 collective-permute-start.27
  50.3 5.5 %collective-permute-done.27.refs_1_ = bf16[32,1152]{1,0:T(8,128)(2,1)S(1)} collective-permute-done((bf16[32,1152]{1,0:T(8,128)(2,1)S(1)}, bf16[32,1152]{1,0:T(8,128)(2,1)S(1)}, u32[]{:S(2)}, u32[]{:S(2)}) %collective-permute-start.27) | collective-permute-done | bytes 73760 | tf_op jit(solution)/shard_map/ppermute | solution.py:83
  55.8 0.0 collective-permute-start.28
  55.8 6.1 %collective-permute-done.28.refs_2_ = bf16[32,1152]{1,0:T(8,128)(2,1)S(1)} collective-permute-done((bf16[32,1152]{1,0:T(8,128)(2,1)S(1)}, bf16[32,1152]{1,0:T(8,128)(2,1)S(1)}, u32[]{:S(2)}, u32[]{:S(2)}) %collective-permute-start.28) | collective-permute-done | bytes 73760 | tf_op jit(solution)/shard_map/ppermute | solution.py:83
  61.9 1.2 collective-permute-start.29
  63.1 3.5 %collective-permute-done.29.refs_3_ = bf16[32,1152]{1,0:T(8,128)(2,1)S(1)} collective-permute-done((bf16[32,1152]{1,0:T(8,128)(2,1)S(1)}, bf16[32,1152]{1,0:T(8,128)(2,1)S(1)}, u32[]{:S(2)}, u32[]{:S(2)}) %collective-permute-start.29) | collective-permute-done | bytes 73760 | tf_op jit(solution)/shard_map/ppermute | solution.py:83
  66.6 0.7 collective-permute-start.30
  67.3 3.8 %collective-permute-done.30.refs_1_ = bf16[32,1152]{1,0:T(8,128)(2,1)S(1)} collective-permute-done((bf16[32,1152]{1,0:T(8,128)(2,1)S(1)}, bf16[32,1152]{1,0:T(8,128)(2,1)S(1)}, u32[]{:S(2)}, u32[]{:S(2)}) %collective-permute-start.30) | collective-permute-done | bytes 73760 | tf_op jit(solution)/shard_map/ppermute | solution.py:83
  71.1 0.9 collective-permute-start.31
  72.0 2.3 %collective-permute-done.31.refs_2_ = bf16[32,1152]{1,0:T(8,128)(2,1)S(1)} collective-permute-done((bf16[32,1152]{1,0:T(8,128)(2,1)S(1)}, bf16[32,1152]{1,0:T(8,128)(2,1)S(1)}, u32[]{:S(2)}, u32[]{:S(2)}) %collective-permute-start.31) | collective-permute-done | bytes 73760 | tf_op jit(solution)/shard_map/ppermute | solution.py:83
  74.3 2.0 %collective-permute-start.32 = (bf16[32,1152]{1,0:T(8,128)(2,1)S(1)}, bf16[32,1152]{1,0:T(8,128)(2,1)S(1)}, u32[]{:S(2)}, u32[]{:S(2)}) collective-permute-start(bf16[32,1152]{1,0:T(8,128)(2,1)S(1)} %shard_map.101.refs_0_), channel_id=1, source_target_pairs={{0,64},{1,65},{2,66},{3,67},{4,68},{5,69},{6,70},{7,71},{8,72},{9,... | collective-permute-start | bytes 221192 | tf_op jit(solution)/shard_map/ppermute | solution.py:83
  76.3 2.7 %collective-permute-done.32.refs_3_ = bf16[32,1152]{1,0:T(8,128)(2,1)S(1)} collective-permute-done((bf16[32,1152]{1,0:T(8,128)(2,1)S(1)}, bf16[32,1152]{1,0:T(8,128)(2,1)S(1)}, u32[]{:S(2)}, u32[]{:S(2)}) %collective-permute-start.32) | collective-permute-done | bytes 73760 | tf_op jit(solution)/shard_map/ppermute | solution.py:83
  79.1 11.7 %collective-permute-start.33 = (f32[32,1152]{1,0:T(8,128)S(1)}, f32[32,1152]{1,0:T(8,128)S(1)}, u32[]{:S(2)}, u32[]{:S(2)}) collective-permute-start(f32[32,1152]{1,0:T(8,128)S(1)} %shard_map.102.mine_ref), channel_id=1, source_target_pairs={{0,8},{1,9},{2,10},{3,11},{4,12},{5,13},{6,14},{7,15},{8,0},{9,1},... | collective-permute-start | bytes 442376 | tf_op jit(solution)/shard_map/ppermute | solution.py:83
  90.9 0.0 collective-permute-done.22.refs_1_
  90.9 0.1 collective-permute-start.20
  91.0 0.0 collective-permute-done.19.refs_1_
  91.0 0.4 collective-permute-start.21
  91.4 0.5 collective-permute-done.33.theirs_ref
  91.9 2.7 %collective-permute-start.15 = (bf16[512,1024]{1,0:T(8,128)(2,1)S(1)}, bf16[512,1024]{1,0:T(8,128)(2,1)S(1)}, u32[]{:S(2)}, u32[]{:S(2)}) collective-permute-start(bf16[512,1024]{1,0:T(8,128)(2,1)S(1)} %collective-permute-done.refs_0_), channel_id=1, source_target_pairs={{0,32},{1,33},{2,34},{3,35},{4,36},{5,37},{6,38},{7,39},{8,104},{9... | collective-permute-start | bytes 3145736 | tf_op jit(solution)/shard_map/ppermute | solution.py:83
  94.6 1.2 collective-permute-start.2
  95.8 0.0 collective-permute-done.4.refs_1_
  95.8 1.1 collective-permute-start.5
  96.8 0.5 collective-permute-start.17
  97.4 9.7 %collective-permute-done.15.refs_2_ = bf16[512,1024]{1,0:T(8,128)(2,1)S(1)} collective-permute-done((bf16[512,1024]{1,0:T(8,128)(2,1)S(1)}, bf16[512,1024]{1,0:T(8,128)(2,1)S(1)}, u32[]{:S(2)}, u32[]{:S(2)}) %collective-permute-start.15) | collective-permute-done | bytes 1048608 | tf_op jit(solution)/shard_map/ppermute | solution.py:83
  107.1 1.5 %collective-permute-done.2.refs_0_ = bf16[512,1024]{1,0:T(8,128)(2,1)S(1)} collective-permute-done((bf16[512,1024]{1,0:T(8,128)(2,1)S(1)}, bf16[512,1024]{1,0:T(8,128)(2,1)S(1)}, u32[]{:S(2)}, u32[]{:S(2)}) %collective-permute-start.2) | collective-permute-done | bytes 1048608 | tf_op jit(solution)/shard_map/ppermute | solution.py:83
  108.5 0.5 collective-permute-start.3
  109.0 9.0 %collective-permute-done.5.refs_1_ = bf16[512,1024]{1,0:T(8,128)(2,1)S(1)} collective-permute-done((bf16[512,1024]{1,0:T(8,128)(2,1)S(1)}, bf16[512,1024]{1,0:T(8,128)(2,1)S(1)}, u32[]{:S(2)}, u32[]{:S(2)}) %collective-permute-start.5) | collective-permute-done | bytes 1048608 | tf_op jit(solution)/shard_map/ppermute | solution.py:83
  118.0 0.2 collective-permute-start.6
  118.3 2.3 %shard_map.94.refs_7_ = bf16[512,8192]{1,0:T(8,128)(2,1)} custom-call(bf16[512,1024]{1,0:T(8,128)(2,1)S(1)} %get-tuple-element.17.refs_0_, bf16[512,1024]{1,0:T(8,128)(2,1)S(1)} %collective-permute-done.22.refs_1_, bf16[512,1024]{1,0:T(8,128)(2,1)S(1)} %copy-done, bf16[512,64]{1,0:T(8,128)(2,1)S(1)} %get-tuple-element.19.refs_3_.refs_5_.refs_7_, ...), custom_call_target="tpu_custom_call" | custom-call | flops 1153433600 | bytes 4200000 | tf_op jit(solution)/shard_map/pallas_call | solution.py:382
  120.6 0.7 in_order.1
  121.3 4.4 %shard_map.95.refs_9_ = bf16[512,8192]{1,0:T(8,128)(2,1)} custom-call(bf16[512,1024]{1,0:T(8,128)(2,1)S(1)} %collective-permute-done.refs_0_, bf16[512,1024]{1,0:T(8,128)(2,1)S(1)} %collective-permute-done.19.refs_1_, bf16[512,1024]{1,0:T(8,128)(2,1)S(1)} %collective-permute-done.20.refs_2_, ...), custom_call_target="tpu_custom_call", output_to_operand_aliasing={{}: (7, {})} | custom-call | flops 2306867200 | bytes 7400000 | tf_op jit(solution)/shard_map/pallas_call | solution.py:382
  125.8 6.4 %shard_map.96.refs_5_ = bf16[512,8192]{1,0:T(8,128)(2,1)} custom-call(bf16[512,1024]{1,0:T(8,128)(2,1)S(1)} %collective-permute-done.1.refs_0_, bf16[512,1024]{1,0:T(8,128)(2,1)S(1)} %collective-permute-done.4.refs_1_, bf16[512,1024]{1,0:T(8,128)(2,1)S(1)} %collective-permute-done.15.refs_2_, ...), custom_call_target="tpu_custom_call", output_to_operand_aliasing={{}: (9, {})} | custom-call | flops 3460300800 | bytes 10600000 | tf_op jit(solution)/shard_map/pallas_call | solution.py:382
  132.2 2.3 %shard_map.97.refs_5_ = bf16[512,8192]{1,0:T(8,128)(2,1)} custom-call(bf16[512,1024]{1,0:T(8,128)(2,1)S(1)} %collective-permute-done.2.refs_0_, bf16[512,1024]{1,0:T(8,128)(2,1)S(1)} %collective-permute-done.5.refs_1_, bf16[512,1024]{1,0:T(8,128)(2,1)S(1)} %copy-done, ...), custom_call_target="tpu_custom_call", output_to_operand_aliasing={{}: (5, {})} | custom-call | flops 1153433600 | bytes 4200000 | tf_op jit(solution)/shard_map/pallas_call | solution.py:382
  134.5 2.3 %shard_map.98 = bf16[512,8192]{1,0:T(8,128)(2,1)} custom-call(bf16[512,1024]{1,0:T(8,128)(2,1)S(1)} %collective-permute-done.3.refs_0_, bf16[512,1024]{1,0:T(8,128)(2,1)S(1)} %collective-permute-done.6.refs_1_, bf16[512,1024]{1,0:T(8,128)(2,1)S(1)} %copy-done, ...), custom_call_target="tpu_custom_call", output_to_operand_aliasing={{}: (5, {})} | custom-call | flops 1153433600 | bytes 4200000 | tf_op jit(solution)/shard_map/pallas_call | solution.py:382
  (21 shorter events, 0.2 us)
Async XLA Ops:
  0.6 29.1 %copy-start = (bf16[512,1024]{1,0:T(8,128)(2,1)S(1)}, bf16[512,1024]{1,0:T(8,128)(2,1)}, u32[]{:S(2)}) copy-start(bf16[512,1024]{1,0:T(8,128)(2,1)} %refs_2_.5) | copy-start | bytes 3145732
  1.6 4.8 %collective-permute-start.7 = (bf16[32,1152]{1,0:T(8,128)(2,1)S(1)}, bf16[32,1152]{1,0:T(8,128)(2,1)S(1)}, u32[]{:S(2)}, u32[]{:S(2)}) collective-permute-start(bf16[32,1152]{1,0:T(8,128)(2,1)S(1)} %pack.1.mine_ref), channel_id=1, source_target_pairs={{0,1},{1,16},{2,3},{3,18},{4,5},{5,20},{6,7},{7,22},{8,25},{9,8},{... | collective-permute-start | bytes 221192 | tf_op jit(solution)/shard_map/ppermute | solution.py:83
  6.4 6.4 %collective-permute-start.9 = (bf16[2,32,1152]{2,1,0:T(8,128)(2,1)S(1)}, bf16[2,32,1152]{2,1,0:T(8,128)(2,1)S(1)}, u32[]{:S(2)}, u32[]{:S(2)}) collective-permute-start(bf16[2,32,1152]{2,1,0:T(8,128)(2,1)S(1)} %join.1.refs_0_), channel_id=1, source_target_pairs={{0,6},{1,7},{2,0},{3,1},{4,2},{5,3},{6,4},{7,5},{8,10},{9,11},{10,... | collective-permute-start | bytes 442376 | tf_op jit(solution)/shard_map/ppermute | solution.py:83
  8.1 11.1 %collective-permute-start.8 = (bf16[2,32,1152]{2,1,0:T(8,128)(2,1)S(1)}, bf16[2,32,1152]{2,1,0:T(8,128)(2,1)S(1)}, u32[]{:S(2)}, u32[]{:S(2)}) collective-permute-start(bf16[2,32,1152]{2,1,0:T(8,128)(2,1)S(1)} %join.1.refs_0_), channel_id=1, source_target_pairs={{0,2},{1,3},{2,4},{3,5},{4,6},{5,7},{6,0},{7,1},{8,14},{9,15},{10,... | collective-permute-start | bytes 442376 | tf_op jit(solution)/shard_map/ppermute | solution.py:83
  12.8 7.5 %collective-permute-start.10 = (bf16[2,32,1152]{2,1,0:T(8,128)(2,1)S(1)}, bf16[2,32,1152]{2,1,0:T(8,128)(2,1)S(1)}, u32[]{:S(2)}, u32[]{:S(2)}) collective-permute-start(bf16[2,32,1152]{2,1,0:T(8,128)(2,1)S(1)} %collective-permute-done.9.refs_2_), channel_id=1, source_target_pairs={{0,6},{1,7},{2,0},{3,1},{4,2},{5,3},{6,4},{7,5},{8,10},{9,11},{10,... | collective-permute-start | bytes 442376 | tf_op jit(solution)/shard_map/ppermute | solution.py:83
  12.8 16.9 %collective-permute-start.11 = (bf16[2,32,1152]{2,1,0:T(8,128)(2,1)S(1)}, bf16[2,32,1152]{2,1,0:T(8,128)(2,1)S(1)}, u32[]{:S(2)}, u32[]{:S(2)}) collective-permute-start(bf16[2,32,1152]{2,1,0:T(8,128)(2,1)S(1)} %join.1.refs_0_), channel_id=1, source_target_pairs={{0,8},{1,9},{2,10},{3,11},{4,12},{5,13},{6,14},{7,15},{8,0},{9,1},... | collective-permute-start | bytes 442376 | tf_op jit(solution)/shard_map/ppermute | solution.py:83
  19.2 10.5 %collective-permute-start.12 = (bf16[2,32,1152]{2,1,0:T(8,128)(2,1)S(1)}, bf16[2,32,1152]{2,1,0:T(8,128)(2,1)S(1)}, u32[]{:S(2)}, u32[]{:S(2)}) collective-permute-start(bf16[2,32,1152]{2,1,0:T(8,128)(2,1)S(1)} %collective-permute-done.9.refs_2_), channel_id=1, source_target_pairs={{0,8},{1,9},{2,10},{3,11},{4,12},{5,13},{6,14},{7,15},{8,0},{9,1},... | collective-permute-start | bytes 442376 | tf_op jit(solution)/shard_map/ppermute | solution.py:83
  19.2 10.5 %collective-permute-start.13 = (bf16[2,32,1152]{2,1,0:T(8,128)(2,1)S(1)}, bf16[2,32,1152]{2,1,0:T(8,128)(2,1)S(1)}, u32[]{:S(2)}, u32[]{:S(2)}) collective-permute-start(bf16[2,32,1152]{2,1,0:T(8,128)(2,1)S(1)} %collective-permute-done.8.refs_1_), channel_id=1, source_target_pairs={{0,8},{1,9},{2,10},{3,11},{4,12},{5,13},{6,14},{7,15},{8,0},{9,1},... | collective-permute-start | bytes 442376 | tf_op jit(solution)/shard_map/ppermute | solution.py:83
  20.2 9.5 %collective-permute-start.14 = (bf16[2,32,1152]{2,1,0:T(8,128)(2,1)S(1)}, bf16[2,32,1152]{2,1,0:T(8,128)(2,1)S(1)}, u32[]{:S(2)}, u32[]{:S(2)}) collective-permute-start(bf16[2,32,1152]{2,1,0:T(8,128)(2,1)S(1)} %collective-permute-done.10.refs_3_), channel_id=1, source_target_pairs={{0,8},{1,9},{2,10},{3,11},{4,12},{5,13},{6,14},{7,15},{8,0},{9,1},... | collective-permute-start | bytes 442376 | tf_op jit(solution)/shard_map/ppermute | solution.py:83
  26.2 18.3 %collective-permute-start = (bf16[512,1024]{1,0:T(8,128)(2,1)S(1)}, bf16[512,1024]{1,0:T(8,128)(2,1)S(1)}, u32[]{:S(2)}, u32[]{:S(2)}) collective-permute-start(bf16[512,1024]{1,0:T(8,128)(2,1)S(1)} %get-tuple-element.17.refs_0_), channel_id=1, source_target_pairs={{0,2},{1,3},{2,4},{3,5},{4,6},{5,7},{6,0},{7,1},{8,14},{9,15},{10,... | collective-permute-start | bytes 3145736 | tf_op jit(solution)/shard_map/ppermute | solution.py:83
  34.6 2.5 %collective-permute-start.23 = (bf16[4,2,32,1152]{3,2,1,0:T(8,128)(2,1)S(1)}, bf16[4,2,32,1152]{3,2,1,0:T(8,128)(2,1)S(1)}, u32[]{:S(2)}, u32[]{:S(2)}) collective-permute-start(bf16[4,2,32,1152]{3,2,1,0:T(8,128)(2,1)S(1)} %get-tuple-element.22), channel_id=1, source_target_pairs={{0,8},{1,9},{2,10},{3,11},{4,12},{5,13},{6,14},{7,15},{8,0},{9,1},... | collective-permute-start | bytes 1769480 | tf_op jit(solution)/shard_map/ppermute | solution.py:83
  34.7 56.1 %collective-permute-start.22 = (bf16[512,1024]{1,0:T(8,128)(2,1)S(1)}, bf16[512,1024]{1,0:T(8,128)(2,1)S(1)}, u32[]{:S(2)}, u32[]{:S(2)}) collective-permute-start(bf16[512,1024]{1,0:T(8,128)(2,1)S(1)} %get-tuple-element.17.refs_0_), channel_id=1, source_target_pairs={{0,8},{1,9},{2,10},{3,11},{4,12},{5,13},{6,14},{7,15},{8,0},{9,1},... | collective-permute-start | bytes 3145736 | tf_op jit(solution)/shard_map/ppermute | solution.py:83
  35.2 55.8 %collective-permute-start.19 = (bf16[512,1024]{1,0:T(8,128)(2,1)S(1)}, bf16[512,1024]{1,0:T(8,128)(2,1)S(1)}, u32[]{:S(2)}, u32[]{:S(2)}) collective-permute-start(bf16[512,1024]{1,0:T(8,128)(2,1)S(1)} %get-tuple-element.17.refs_0_), channel_id=1, source_target_pairs={{0,1},{1,16},{2,3},{3,18},{4,5},{5,20},{6,7},{7,22},{8,25},{9,8},{... | collective-permute-start | bytes 3145736 | tf_op jit(solution)/shard_map/ppermute | solution.py:83
  37.2 7.1 %collective-permute-start.25 = (bf16[2,32,1152]{2,1,0:T(8,128)(2,1)S(1)}, bf16[2,32,1152]{2,1,0:T(8,128)(2,1)S(1)}, u32[]{:S(2)}, u32[]{:S(2)}) collective-permute-start(bf16[2,32,1152]{2,1,0:T(8,128)(2,1)S(1)} %get-tuple-element.26), channel_id=1, source_target_pairs={{0,6},{1,7},{2,0},{3,1},{4,2},{5,3},{6,4},{7,5},{8,10},{9,11},{10,... | collective-permute-start | bytes 442376 | tf_op jit(solution)/shard_map/ppermute | solution.py:83
  37.3 9.9 %collective-permute-start.24 = (bf16[2,32,1152]{2,1,0:T(8,128)(2,1)S(1)}, bf16[2,32,1152]{2,1,0:T(8,128)(2,1)S(1)}, u32[]{:S(2)}, u32[]{:S(2)}) collective-permute-start(bf16[2,32,1152]{2,1,0:T(8,128)(2,1)S(1)} %get-tuple-element.24), channel_id=1, source_target_pairs={{0,2},{1,3},{2,4},{3,5},{4,6},{5,7},{6,0},{7,1},{8,14},{9,15},{10,... | collective-permute-start | bytes 442376 | tf_op jit(solution)/shard_map/ppermute | solution.py:83
  44.4 5.7 %collective-permute-start.26 = (bf16[2,32,1152]{2,1,0:T(8,128)(2,1)S(1)}, bf16[2,32,1152]{2,1,0:T(8,128)(2,1)S(1)}, u32[]{:S(2)}, u32[]{:S(2)}) collective-permute-start(bf16[2,32,1152]{2,1,0:T(8,128)(2,1)S(1)} %shard_map.99), channel_id=1, source_target_pairs={{0,6},{1,7},{2,0},{3,1},{4,2},{5,3},{6,4},{7,5},{8,10},{9,11},{10,... | collective-permute-start | bytes 442376 | tf_op jit(solution)/shard_map/ppermute | solution.py:83
  44.5 50.1 %collective-permute-start.1 = (bf16[512,1024]{1,0:T(8,128)(2,1)S(1)}, bf16[512,1024]{1,0:T(8,128)(2,1)S(1)}, u32[]{:S(2)}, u32[]{:S(2)}) collective-permute-start(bf16[512,1024]{1,0:T(8,128)(2,1)S(1)} %collective-permute-done.refs_0_), channel_id=1, source_target_pairs={{0,2},{1,3},{2,4},{3,5},{4,6},{5,7},{6,0},{7,1},{8,14},{9,15},{10,... | collective-permute-start | bytes 3145736 | tf_op jit(solution)/shard_map/ppermute | solution.py:83
  47.2 48.6 %collective-permute-start.4 = (bf16[512,1024]{1,0:T(8,128)(2,1)S(1)}, bf16[512,1024]{1,0:T(8,128)(2,1)S(1)}, u32[]{:S(2)}, u32[]{:S(2)}) collective-permute-start(bf16[512,1024]{1,0:T(8,128)(2,1)S(1)} %collective-permute-done.refs_0_), channel_id=1, source_target_pairs={{0,1},{1,16},{2,3},{3,18},{4,5},{5,20},{6,7},{7,22},{8,25},{9,8},{... | collective-permute-start | bytes 3145736 | tf_op jit(solution)/shard_map/ppermute | solution.py:83
  50.2 5.6 %collective-permute-start.27 = (bf16[32,1152]{1,0:T(8,128)(2,1)S(1)}, bf16[32,1152]{1,0:T(8,128)(2,1)S(1)}, u32[]{:S(2)}, u32[]{:S(2)}) collective-permute-start(bf16[32,1152]{1,0:T(8,128)(2,1)S(1)} %get-tuple-element.28), channel_id=1, source_target_pairs={{0,1},{1,16},{2,3},{3,18},{4,5},{5,20},{6,7},{7,22},{8,9},{9,24},{... | collective-permute-start | bytes 221192 | tf_op jit(solution)/shard_map/ppermute | solution.py:83
  55.8 6.1 %collective-permute-start.28 = (bf16[32,1152]{1,0:T(8,128)(2,1)S(1)}, bf16[32,1152]{1,0:T(8,128)(2,1)S(1)}, u32[]{:S(2)}, u32[]{:S(2)}) collective-permute-start(bf16[32,1152]{1,0:T(8,128)(2,1)S(1)} %get-tuple-element.28), channel_id=1, source_target_pairs={{0,17},{1,0},{2,19},{3,2},{4,21},{5,4},{6,23},{7,6},{8,25},{9,8},{... | collective-permute-start | bytes 221192 | tf_op jit(solution)/shard_map/ppermute | solution.py:83
  61.9 4.7 %collective-permute-start.29 = (bf16[32,1152]{1,0:T(8,128)(2,1)S(1)}, bf16[32,1152]{1,0:T(8,128)(2,1)S(1)}, u32[]{:S(2)}, u32[]{:S(2)}) collective-permute-start(bf16[32,1152]{1,0:T(8,128)(2,1)S(1)} %get-tuple-element.27.refs_0_), channel_id=1, source_target_pairs={{0,16},{1,17},{2,18},{3,19},{4,20},{5,21},{6,22},{7,23},{8,24},{9,... | collective-permute-start | bytes 221192 | tf_op jit(solution)/shard_map/ppermute | solution.py:83
  66.6 4.5 %collective-permute-start.30 = (bf16[32,1152]{1,0:T(8,128)(2,1)S(1)}, bf16[32,1152]{1,0:T(8,128)(2,1)S(1)}, u32[]{:S(2)}, u32[]{:S(2)}) collective-permute-start(bf16[32,1152]{1,0:T(8,128)(2,1)S(1)} %shard_map.101.refs_0_), channel_id=1, source_target_pairs={{0,32},{1,33},{2,34},{3,35},{4,36},{5,37},{6,38},{7,39},{8,40},{9,... | collective-permute-start | bytes 221192 | tf_op jit(solution)/shard_map/ppermute | solution.py:83
  71.1 3.2 %collective-permute-start.31 = (bf16[32,1152]{1,0:T(8,128)(2,1)S(1)}, bf16[32,1152]{1,0:T(8,128)(2,1)S(1)}, u32[]{:S(2)}, u32[]{:S(2)}) collective-permute-start(bf16[32,1152]{1,0:T(8,128)(2,1)S(1)} %shard_map.101.refs_0_), channel_id=1, source_target_pairs={{0,96},{1,97},{2,98},{3,99},{4,100},{5,101},{6,102},{7,103},{8,104... | collective-permute-start | bytes 221192 | tf_op jit(solution)/shard_map/ppermute | solution.py:83
  74.3 4.7 %collective-permute-start.32 = (bf16[32,1152]{1,0:T(8,128)(2,1)S(1)}, bf16[32,1152]{1,0:T(8,128)(2,1)S(1)}, u32[]{:S(2)}, u32[]{:S(2)}) collective-permute-start(bf16[32,1152]{1,0:T(8,128)(2,1)S(1)} %shard_map.101.refs_0_), channel_id=1, source_target_pairs={{0,64},{1,65},{2,66},{3,67},{4,68},{5,69},{6,70},{7,71},{8,72},{9,... | collective-permute-start | bytes 221192 | tf_op jit(solution)/shard_map/ppermute | solution.py:83
  79.1 12.8 %collective-permute-start.33 = (f32[32,1152]{1,0:T(8,128)S(1)}, f32[32,1152]{1,0:T(8,128)S(1)}, u32[]{:S(2)}, u32[]{:S(2)}) collective-permute-start(f32[32,1152]{1,0:T(8,128)S(1)} %shard_map.102.mine_ref), channel_id=1, source_target_pairs={{0,8},{1,9},{2,10},{3,11},{4,12},{5,13},{6,14},{7,15},{8,0},{9,1},... | collective-permute-start | bytes 442376 | tf_op jit(solution)/shard_map/ppermute | solution.py:83
  90.9 6.0 %collective-permute-start.20 = (bf16[512,1024]{1,0:T(8,128)(2,1)S(1)}, bf16[512,1024]{1,0:T(8,128)(2,1)S(1)}, u32[]{:S(2)}, u32[]{:S(2)}) collective-permute-start(bf16[512,1024]{1,0:T(8,128)(2,1)S(1)} %collective-permute-done.refs_0_), channel_id=1, source_target_pairs={{0,8},{1,9},{2,10},{3,11},{4,12},{5,13},{6,14},{7,15},{8,0},{9,1},... | collective-permute-start | bytes 3145736 | tf_op jit(solution)/shard_map/ppermute | solution.py:83
  91.0 5.9 %collective-permute-start.21 = (bf16[512,1024]{1,0:T(8,128)(2,1)S(1)}, bf16[512,1024]{1,0:T(8,128)(2,1)S(1)}, u32[]{:S(2)}, u32[]{:S(2)}) collective-permute-start(bf16[512,1024]{1,0:T(8,128)(2,1)S(1)} %collective-permute-done.19.refs_1_), channel_id=1, source_target_pairs={{0,8},{1,9},{2,10},{3,11},{4,12},{5,13},{6,14},{7,15},{8,0},{9,1},... | collective-permute-start | bytes 3145736 | tf_op jit(solution)/shard_map/ppermute | solution.py:83
  91.9 15.2 %collective-permute-start.15 = (bf16[512,1024]{1,0:T(8,128)(2,1)S(1)}, bf16[512,1024]{1,0:T(8,128)(2,1)S(1)}, u32[]{:S(2)}, u32[]{:S(2)}) collective-permute-start(bf16[512,1024]{1,0:T(8,128)(2,1)S(1)} %collective-permute-done.refs_0_), channel_id=1, source_target_pairs={{0,32},{1,33},{2,34},{3,35},{4,36},{5,37},{6,38},{7,39},{8,104},{9... | collective-permute-start | bytes 3145736 | tf_op jit(solution)/shard_map/ppermute | solution.py:83
  94.6 13.9 %collective-permute-start.2 = (bf16[512,1024]{1,0:T(8,128)(2,1)S(1)}, bf16[512,1024]{1,0:T(8,128)(2,1)S(1)}, u32[]{:S(2)}, u32[]{:S(2)}) collective-permute-start(bf16[512,1024]{1,0:T(8,128)(2,1)S(1)} %collective-permute-done.1.refs_0_), channel_id=1, source_target_pairs={{0,1},{1,16},{2,3},{3,18},{4,5},{5,20},{6,7},{7,22},{8,25},{9,8},{... | collective-permute-start | bytes 3145736 | tf_op jit(solution)/shard_map/ppermute | solution.py:83
  95.8 22.2 %collective-permute-start.5 = (bf16[512,1024]{1,0:T(8,128)(2,1)S(1)}, bf16[512,1024]{1,0:T(8,128)(2,1)S(1)}, u32[]{:S(2)}, u32[]{:S(2)}) collective-permute-start(bf16[512,1024]{1,0:T(8,128)(2,1)S(1)} %collective-permute-done.4.refs_1_), channel_id=1, source_target_pairs={{0,32},{1,33},{2,34},{3,35},{4,36},{5,37},{6,38},{7,39},{8,104},{9... | collective-permute-start | bytes 3145736 | tf_op jit(solution)/shard_map/ppermute | solution.py:83
  96.8 28.9 %collective-permute-start.16 = (bf16[512,1024]{1,0:T(8,128)(2,1)S(1)}, bf16[512,1024]{1,0:T(8,128)(2,1)S(1)}, u32[]{:S(2)}, u32[]{:S(2)}) collective-permute-start(bf16[512,1024]{1,0:T(8,128)(2,1)S(1)} %collective-permute-done.1.refs_0_), channel_id=1, source_target_pairs={{0,8},{1,9},{2,10},{3,11},{4,12},{5,13},{6,14},{7,15},{8,0},{9,1},... | collective-permute-start | bytes 3145736 | tf_op jit(solution)/shard_map/ppermute | solution.py:83
  96.8 28.9 %collective-permute-start.17 = (bf16[512,1024]{1,0:T(8,128)(2,1)S(1)}, bf16[512,1024]{1,0:T(8,128)(2,1)S(1)}, u32[]{:S(2)}, u32[]{:S(2)}) collective-permute-start(bf16[512,1024]{1,0:T(8,128)(2,1)S(1)} %collective-permute-done.4.refs_1_), channel_id=1, source_target_pairs={{0,8},{1,9},{2,10},{3,11},{4,12},{5,13},{6,14},{7,15},{8,0},{9,1},... | collective-permute-start | bytes 3145736 | tf_op jit(solution)/shard_map/ppermute | solution.py:83
  107.1 18.7 %collective-permute-start.18 = (bf16[512,1024]{1,0:T(8,128)(2,1)S(1)}, bf16[512,1024]{1,0:T(8,128)(2,1)S(1)}, u32[]{:S(2)}, u32[]{:S(2)}) collective-permute-start(bf16[512,1024]{1,0:T(8,128)(2,1)S(1)} %collective-permute-done.15.refs_2_), channel_id=1, source_target_pairs={{0,8},{1,9},{2,10},{3,11},{4,12},{5,13},{6,14},{7,15},{8,0},{9,1},... | collective-permute-start | bytes 3145736 | tf_op jit(solution)/shard_map/ppermute | solution.py:83
  108.5 26.0 %collective-permute-start.3 = (bf16[512,1024]{1,0:T(8,128)(2,1)S(1)}, bf16[512,1024]{1,0:T(8,128)(2,1)S(1)}, u32[]{:S(2)}, u32[]{:S(2)}) collective-permute-start(bf16[512,1024]{1,0:T(8,128)(2,1)S(1)} %collective-permute-done.2.refs_0_), channel_id=1, source_target_pairs={{0,8},{1,9},{2,10},{3,11},{4,12},{5,13},{6,14},{7,15},{8,0},{9,1},... | collective-permute-start | bytes 3145736 | tf_op jit(solution)/shard_map/ppermute | solution.py:83
  118.0 16.5 %collective-permute-start.6 = (bf16[512,1024]{1,0:T(8,128)(2,1)S(1)}, bf16[512,1024]{1,0:T(8,128)(2,1)S(1)}, u32[]{:S(2)}, u32[]{:S(2)}) collective-permute-start(bf16[512,1024]{1,0:T(8,128)(2,1)S(1)} %collective-permute-done.5.refs_1_), channel_id=1, source_target_pairs={{0,8},{1,9},{2,10},{3,11},{4,12},{5,13},{6,14},{7,15},{8,0},{9,1},... | collective-permute-start | bytes 3145736 | tf_op jit(solution)/shard_map/ppermute | solution.py:83

commit v3 on v2

--- a/solution.py
+++ b/solution.py
@@ -74,6 +74,11 @@
     return x, (y + step) % 4, z, core
 
 
+def y_other(x, y, z, core):
+    step = -1 if (core + y) % 2 == 0 else 1
+    return x, (y + step) % 4, z, core
+
+
 def core_swap(x, y, z, core):
     return x, y, z, 1 - core
 
@@ -461,11 +466,11 @@
     for by, part in ((1, cross), (3, cross), (2, mine)):
         parts.append(moved(part, shifted("x", by)))
     mine = sums_of(parts, jnp.bfloat16)
-    parts = [mine]
-    for by in (1, 3, 2):
-        parts.append(moved(mine, shifted("y", by)))
+    arrived = moved(mine, y_other)
+    mine = sums_of((mine, arrived), jnp.bfloat16)
+    arrived = moved(mine, y_swap)
     scale = adapter_scale * float(TOKENS * DEVICES) ** (-0.5)
-    mine = sums_of(parts, jnp.float32, scale=scale)
+    mine = sums_of((mine, arrived), jnp.float32, scale=scale)
 
     pieces = (w, w_z1, w_x0, w_z2, w_x1, w_y1, w_x2, w_xy)
     mirrored = []

time: 137 us -> 131 us (0.956)
  starting transfers between devices: 52.5 us -> 49.5 us
  waiting for transfers between devices: 54.4 us -> 51.7 us
    ppermute x34 -> x33, starting transfers between devices: 52.5 us -> 49.5 us  [moved(): return lax.ppermute(value, AXES, pairs)]
    ppermute x34 -> x33, waiting for transfers between devices: 54.4 us -> 51.7 us  [moved(): return lax.ppermute(value, AXES, pairs)]
  transfers between devices with their start and end apart: 34 -> 33, of which waited for: 14 -> 13; matrix products, arithmetic and copies ran while one was open for 0% -> 0% of each run, Pallas kernels for 19% -> 20%
where the time goes in v3:
time: 131 us
  waiting for transfers between devices  51.7 us (39%)
  starting transfers between devices  49.5 us (38%)
  Pallas kernels  29 us (22%)
    ppermute x33, waiting for transfers between devices, moved(): return lax.ppermute(value, AXES, pairs)  51.7 us
    ppermute x33, starting transfers between devices, moved(): return lax.ppermute(value, AXES, pairs)  49.5 us
    pallas_call x5, Pallas kernels, product(): pl.pallas_call(functools.partial(product_kernel, slots, aliased), in_spec...  17.8 us
    pallas_call x1, Pallas kernels, adapter_terms(): pl.pallas_call(adapter_kernel, in_specs=[VMEM] * 10, out_specs=[VMEM] * 4...  4.89 us
    pallas_call x1, Pallas kernels, prepared(): pl.pallas_call(prepare_kernel, in_specs=[HBM, HBM, HBM, HBM], out_specs=[...  4.33 us
  transfers between devices with their start and end apart: 33, of which 13 were waited for; matrix products, arithmetic and copies ran while one was open for 0% of the time, Pallas kernels for 20%

profile of v3, /device:TPU:1, one launch (start us, length us, event | category | flops | bytes accessed | tf_op | source)
XLA Modules:
  0.0 131.2 jit_solution(15828298299294735136)
XLA Ops:
  0.6 1.0 pack.1.mine_ref
  1.6 3.4 %collective-permute-start.7 = (bf16[32,1152]{1,0:T(8,128)(2,1)S(1)}, bf16[32,1152]{1,0:T(8,128)(2,1)S(1)}, u32[]{:S(2)}, u32[]{:S(2)}) collective-permute-start(bf16[32,1152]{1,0:T(8,128)(2,1)S(1)} %pack.1.mine_ref), channel_id=1, source_target_pairs={{0,1},{1,16},{2,3},{3,18},{4,5},{5,20},{6,7},{7,22},{8,25},{9,8},{... | collective-permute-start | bytes 221192 | tf_op jit(solution)/shard_map/ppermute | solution.py:88
  5.0 1.4 %collective-permute-done.7.crossed_ref = bf16[32,1152]{1,0:T(8,128)(2,1)S(1)} collective-permute-done((bf16[32,1152]{1,0:T(8,128)(2,1)S(1)}, bf16[32,1152]{1,0:T(8,128)(2,1)S(1)}, u32[]{:S(2)}, u32[]{:S(2)}) %collective-permute-start.7) | collective-permute-done | bytes 73760 | tf_op jit(solution)/shard_map/ppermute | solution.py:88
  6.4 1.7 %collective-permute-start.9 = (bf16[2,32,1152]{2,1,0:T(8,128)(2,1)S(1)}, bf16[2,32,1152]{2,1,0:T(8,128)(2,1)S(1)}, u32[]{:S(2)}, u32[]{:S(2)}) collective-permute-start(bf16[2,32,1152]{2,1,0:T(8,128)(2,1)S(1)} %join.1.refs_0_), channel_id=1, source_target_pairs={{0,6},{1,7},{2,0},{3,1},{4,2},{5,3},{6,4},{7,5},{8,10},{9,11},{10,... | collective-permute-start | bytes 442376 | tf_op jit(solution)/shard_map/ppermute | solution.py:88
  8.1 2.2 %collective-permute-start.8 = (bf16[2,32,1152]{2,1,0:T(8,128)(2,1)S(1)}, bf16[2,32,1152]{2,1,0:T(8,128)(2,1)S(1)}, u32[]{:S(2)}, u32[]{:S(2)}) collective-permute-start(bf16[2,32,1152]{2,1,0:T(8,128)(2,1)S(1)} %join.1.refs_0_), channel_id=1, source_target_pairs={{0,2},{1,3},{2,4},{3,5},{4,6},{5,7},{6,0},{7,1},{8,14},{9,15},{10,... | collective-permute-start | bytes 442376 | tf_op jit(solution)/shard_map/ppermute | solution.py:88
  10.3 2.5 %collective-permute-done.9.refs_2_ = bf16[2,32,1152]{2,1,0:T(8,128)(2,1)S(1)} collective-permute-done((bf16[2,32,1152]{2,1,0:T(8,128)(2,1)S(1)}, bf16[2,32,1152]{2,1,0:T(8,128)(2,1)S(1)}, u32[]{:S(2)}, u32[]{:S(2)}) %collective-permute-start.9) | collective-permute-done | bytes 147488 | tf_op jit(solution)/shard_map/ppermute | solution.py:88
  12.8 6.4 %collective-permute-start.11 = (bf16[2,32,1152]{2,1,0:T(8,128)(2,1)S(1)}, bf16[2,32,1152]{2,1,0:T(8,128)(2,1)S(1)}, u32[]{:S(2)}, u32[]{:S(2)}) collective-permute-start(bf16[2,32,1152]{2,1,0:T(8,128)(2,1)S(1)} %join.1.refs_0_), channel_id=1, source_target_pairs={{0,8},{1,9},{2,10},{3,11},{4,12},{5,13},{6,14},{7,15},{8,0},{9,1},... | collective-permute-start | bytes 442376 | tf_op jit(solution)/shard_map/ppermute | solution.py:88
  19.2 0.0 collective-permute-start.12
  19.2 0.0 collective-permute-done.8.refs_1_
  19.2 1.0 collective-permute-start.13
  20.2 1.7 %collective-permute-start.14 = (bf16[2,32,1152]{2,1,0:T(8,128)(2,1)S(1)}, bf16[2,32,1152]{2,1,0:T(8,128)(2,1)S(1)}, u32[]{:S(2)}, u32[]{:S(2)}) collective-permute-start(bf16[2,32,1152]{2,1,0:T(8,128)(2,1)S(1)} %collective-permute-done.10.refs_3_), channel_id=1, source_target_pairs={{0,8},{1,9},{2,10},{3,11},{4,12},{5,13},{6,14},{7,15},{8,0},{9,1},... | collective-permute-start | bytes 442376 | tf_op jit(solution)/shard_map/ppermute | solution.py:88
  21.9 4.3 %prepare.1 = (bf16[512,1024]{1,0:T(8,128)(2,1)S(1)}, bf16[512,8192]{1,0:T(8,128)(2,1)S(1)}) custom-call(s32[16,16,1024]{2,1,0:T(8,128)} %codes_ref.1, s32[16,1024]{1,0:T(8,128)} %scale_ref.1, f32[1,1024]{1,0:T(1,128)} %bitcast.1, bf16[512,8192]{1,0:T(8,128)(2,1)} %acts_ref.1), custom_call_target="tpu_custom_call" | custom-call | flops 2000000000 | bytes 9600000 | tf_op jit(solution)/shard_map/prepare/pallas_call | solution.py:222
  26.2 3.5 %collective-permute-start = (bf16[512,1024]{1,0:T(8,128)(2,1)S(1)}, bf16[512,1024]{1,0:T(8,128)(2,1)S(1)}, u32[]{:S(2)}, u32[]{:S(2)}) collective-permute-start(bf16[512,1024]{1,0:T(8,128)(2,1)S(1)} %get-tuple-element.17.refs_0_), channel_id=1, source_target_pairs={{0,2},{1,3},{2,4},{3,5},{4,6},{5,7},{6,0},{7,1},{8,14},{9,15},{10,... | collective-permute-start | bytes 3145736 | tf_op jit(solution)/shard_map/ppermute | solution.py:88
  29.7 0.0 collective-permute-done.11.refs_4_
  29.7 0.0 collective-permute-done.14.refs_7_
  29.7 4.9 %adapter.1 = (bf16[512,64]{1,0:T(8,128)(2,1)S(1)}, bf16[4,2,64,1024]{3,2,1,0:T(8,128)(2,1)S(1)}, bf16[4,2,32,1152]{3,2,1,0:T(8,128)(2,1)S(1)}, bf16[4,2,32,1152]{3,2,1,0:T(8,128)(2,1)S(1)}) custom-call(bf16[512,1024]{1,0:T(8,128)(2,1)S(1)} %copy-done, bf16[2,32,1152]{2,1,0:T(8,128)(2,1)S(1)} %join.1.refs_0_, ...), custom_call_target="tpu_custom_call" | custom-call | flops 5000000000 | bytes 12000000 | tf_op jit(solution)/shard_map/adapter/pallas_call | solution.py:297
  34.6 0.1 collective-permute-start.23
  34.7 0.5 collective-permute-start.22
  35.2 1.9 %collective-permute-start.19 = (bf16[512,1024]{1,0:T(8,128)(2,1)S(1)}, bf16[512,1024]{1,0:T(8,128)(2,1)S(1)}, u32[]{:S(2)}, u32[]{:S(2)}) collective-permute-start(bf16[512,1024]{1,0:T(8,128)(2,1)S(1)} %get-tuple-element.17.refs_0_), channel_id=1, source_target_pairs={{0,1},{1,16},{2,3},{3,18},{4,5},{5,20},{6,7},{7,22},{8,25},{9,8},{... | collective-permute-start | bytes 3145736 | tf_op jit(solution)/shard_map/ppermute | solution.py:88
  37.1 0.0 collective-permute-done.23.arrived_ref
  37.1 0.1 core_sums.1
  37.2 0.1 collective-permute-start.25
  37.3 2.7 %collective-permute-start.24 = (bf16[2,32,1152]{2,1,0:T(8,128)(2,1)S(1)}, bf16[2,32,1152]{2,1,0:T(8,128)(2,1)S(1)}, u32[]{:S(2)}, u32[]{:S(2)}) collective-permute-start(bf16[2,32,1152]{2,1,0:T(8,128)(2,1)S(1)} %get-tuple-element.24), channel_id=1, source_target_pairs={{0,2},{1,3},{2,4},{3,5},{4,6},{5,7},{6,0},{7,1},{8,14},{9,15},{10,... | collective-permute-start | bytes 442376 | tf_op jit(solution)/shard_map/ppermute | solution.py:88
  40.0 4.4 %collective-permute-done.25.refs_1_ = bf16[2,32,1152]{2,1,0:T(8,128)(2,1)S(1)} collective-permute-done((bf16[2,32,1152]{2,1,0:T(8,128)(2,1)S(1)}, bf16[2,32,1152]{2,1,0:T(8,128)(2,1)S(1)}, u32[]{:S(2)}, u32[]{:S(2)}) %collective-permute-start.25) | collective-permute-done | bytes 147488 | tf_op jit(solution)/shard_map/ppermute | solution.py:88
  44.4 0.1 collective-permute-start.26
  44.5 2.7 %collective-permute-start.1 = (bf16[512,1024]{1,0:T(8,128)(2,1)S(1)}, bf16[512,1024]{1,0:T(8,128)(2,1)S(1)}, u32[]{:S(2)}, u32[]{:S(2)}) collective-permute-start(bf16[512,1024]{1,0:T(8,128)(2,1)S(1)} %collective-permute-done.refs_0_), channel_id=1, source_target_pairs={{0,2},{1,3},{2,4},{3,5},{4,6},{5,7},{6,0},{7,1},{8,14},{9,15},{10,... | collective-permute-start | bytes 3145736 | tf_op jit(solution)/shard_map/ppermute | solution.py:88
  47.2 0.0 collective-permute-done.24.refs_1_
  47.2 1.5 %collective-permute-start.4 = (bf16[512,1024]{1,0:T(8,128)(2,1)S(1)}, bf16[512,1024]{1,0:T(8,128)(2,1)S(1)}, u32[]{:S(2)}, u32[]{:S(2)}) collective-permute-start(bf16[512,1024]{1,0:T(8,128)(2,1)S(1)} %collective-permute-done.refs_0_), channel_id=1, source_target_pairs={{0,1},{1,16},{2,3},{3,18},{4,5},{5,20},{6,7},{7,22},{8,25},{9,8},{... | collective-permute-start | bytes 3145736 | tf_op jit(solution)/shard_map/ppermute | solution.py:88
  48.6 1.5 %collective-permute-done.26.refs_2_ = bf16[2,32,1152]{2,1,0:T(8,128)(2,1)S(1)} collective-permute-done((bf16[2,32,1152]{2,1,0:T(8,128)(2,1)S(1)}, bf16[2,32,1152]{2,1,0:T(8,128)(2,1)S(1)}, u32[]{:S(2)}, u32[]{:S(2)}) %collective-permute-start.26) | collective-permute-done | bytes 147488 | tf_op jit(solution)/shard_map/ppermute | solution.py:88
  50.1 0.1 shard_map.100
  50.2 0.1 collective-permute-start.27
  50.3 5.5 %collective-permute-done.27.refs_1_ = bf16[32,1152]{1,0:T(8,128)(2,1)S(1)} collective-permute-done((bf16[32,1152]{1,0:T(8,128)(2,1)S(1)}, bf16[32,1152]{1,0:T(8,128)(2,1)S(1)}, u32[]{:S(2)}, u32[]{:S(2)}) %collective-permute-start.27) | collective-permute-done | bytes 73760 | tf_op jit(solution)/shard_map/ppermute | solution.py:88
  55.8 0.0 collective-permute-start.28
  55.8 6.1 %collective-permute-done.28.refs_2_ = bf16[32,1152]{1,0:T(8,128)(2,1)S(1)} collective-permute-done((bf16[32,1152]{1,0:T(8,128)(2,1)S(1)}, bf16[32,1152]{1,0:T(8,128)(2,1)S(1)}, u32[]{:S(2)}, u32[]{:S(2)}) %collective-permute-start.28) | collective-permute-done | bytes 73760 | tf_op jit(solution)/shard_map/ppermute | solution.py:88
  61.9 1.2 collective-permute-start.29
  63.1 3.5 %collective-permute-done.29.refs_3_ = bf16[32,1152]{1,0:T(8,128)(2,1)S(1)} collective-permute-done((bf16[32,1152]{1,0:T(8,128)(2,1)S(1)}, bf16[32,1152]{1,0:T(8,128)(2,1)S(1)}, u32[]{:S(2)}, u32[]{:S(2)}) %collective-permute-start.29) | collective-permute-done | bytes 73760 | tf_op jit(solution)/shard_map/ppermute | solution.py:88
  66.6 0.7 collective-permute-start.30
  67.4 2.6 %collective-permute-done.30.refs_1_ = bf16[32,1152]{1,0:T(8,128)(2,1)S(1)} collective-permute-done((bf16[32,1152]{1,0:T(8,128)(2,1)S(1)}, bf16[32,1152]{1,0:T(8,128)(2,1)S(1)}, u32[]{:S(2)}, u32[]{:S(2)}) %collective-permute-start.30) | collective-permute-done | bytes 73760 | tf_op jit(solution)/shard_map/ppermute | solution.py:88
  69.9 2.3 %collective-permute-start.31 = (bf16[32,1152]{1,0:T(8,128)(2,1)S(1)}, bf16[32,1152]{1,0:T(8,128)(2,1)S(1)}, u32[]{:S(2)}, u32[]{:S(2)}) collective-permute-start(bf16[32,1152]{1,0:T(8,128)(2,1)S(1)} %shard_map.102.refs_0_), channel_id=1, source_target_pairs={{0,32},{1,33},{2,34},{3,35},{4,36},{5,37},{6,38},{7,39},{8,104},{9... | collective-permute-start | bytes 221192 | tf_op jit(solution)/shard_map/ppermute | solution.py:88
  72.3 2.3 %collective-permute-done.31.refs_1_ = bf16[32,1152]{1,0:T(8,128)(2,1)S(1)} collective-permute-done((bf16[32,1152]{1,0:T(8,128)(2,1)S(1)}, bf16[32,1152]{1,0:T(8,128)(2,1)S(1)}, u32[]{:S(2)}, u32[]{:S(2)}) %collective-permute-start.31) | collective-permute-done | bytes 73760 | tf_op jit(solution)/shard_map/ppermute | solution.py:88
  74.6 10.4 %collective-permute-start.32 = (f32[32,1152]{1,0:T(8,128)S(1)}, f32[32,1152]{1,0:T(8,128)S(1)}, u32[]{:S(2)}, u32[]{:S(2)}) collective-permute-start(f32[32,1152]{1,0:T(8,128)S(1)} %shard_map.103.mine_ref), channel_id=1, source_target_pairs={{0,8},{1,9},{2,10},{3,11},{4,12},{5,13},{6,14},{7,15},{8,0},{9,1},... | collective-permute-start | bytes 442376 | tf_op jit(solution)/shard_map/ppermute | solution.py:88
  85.1 0.1 collective-permute-start.20
  85.2 0.0 collective-permute-done.19.refs_1_
  85.2 0.4 collective-permute-start.21
  85.6 0.5 collective-permute-done.32.theirs_ref
  86.1 3.0 %collective-permute-start.15 = (bf16[512,1024]{1,0:T(8,128)(2,1)S(1)}, bf16[512,1024]{1,0:T(8,128)(2,1)S(1)}, u32[]{:S(2)}, u32[]{:S(2)}) collective-permute-start(bf16[512,1024]{1,0:T(8,128)(2,1)S(1)} %collective-permute-done.refs_0_), channel_id=1, source_target_pairs={{0,32},{1,33},{2,34},{3,35},{4,36},{5,37},{6,38},{7,39},{8,104},{9... | collective-permute-start | bytes 3145736 | tf_op jit(solution)/shard_map/ppermute | solution.py:88
  89.0 0.0 collective-permute-done.1.refs_0_
  89.0 0.9 collective-permute-start.2
  90.0 0.5 collective-permute-start.5
  90.5 0.0 collective-permute-start.16
  90.5 0.0 collective-permute-done.21.refs_3_
  90.5 0.5 collective-permute-start.17
  91.0 10.5 %collective-permute-done.15.refs_2_ = bf16[512,1024]{1,0:T(8,128)(2,1)S(1)} collective-permute-done((bf16[512,1024]{1,0:T(8,128)(2,1)S(1)}, bf16[512,1024]{1,0:T(8,128)(2,1)S(1)}, u32[]{:S(2)}, u32[]{:S(2)}) %collective-permute-start.15) | collective-permute-done | bytes 1048608 | tf_op jit(solution)/shard_map/ppermute | solution.py:88
  101.5 1.5 %collective-permute-done.2.refs_0_ = bf16[512,1024]{1,0:T(8,128)(2,1)S(1)} collective-permute-done((bf16[512,1024]{1,0:T(8,128)(2,1)S(1)}, bf16[512,1024]{1,0:T(8,128)(2,1)S(1)}, u32[]{:S(2)}, u32[]{:S(2)}) %collective-permute-start.2) | collective-permute-done | bytes 1048608 | tf_op jit(solution)/shard_map/ppermute | solution.py:88
  103.0 0.1 collective-permute-start.3
  103.0 9.4 %collective-permute-done.5.refs_1_ = bf16[512,1024]{1,0:T(8,128)(2,1)S(1)} collective-permute-done((bf16[512,1024]{1,0:T(8,128)(2,1)S(1)}, bf16[512,1024]{1,0:T(8,128)(2,1)S(1)}, u32[]{:S(2)}, u32[]{:S(2)}) %collective-permute-start.5) | collective-permute-done | bytes 1048608 | tf_op jit(solution)/shard_map/ppermute | solution.py:88
  112.4 0.0 collective-permute-start.6
  112.5 2.3 %shard_map.94.refs_7_ = bf16[512,8192]{1,0:T(8,128)(2,1)} custom-call(bf16[512,1024]{1,0:T(8,128)(2,1)S(1)} %get-tuple-element.17.refs_0_, bf16[512,1024]{1,0:T(8,128)(2,1)S(1)} %collective-permute-done.22.refs_1_, bf16[512,1024]{1,0:T(8,128)(2,1)S(1)} %copy-done, bf16[512,64]{1,0:T(8,128)(2,1)S(1)} %get-tuple-element.19.refs_3_.refs_5_.refs_7_, ...), custom_call_target="tpu_custom_call" | custom-call | flops 1153433600 | bytes 4200000 | tf_op jit(solution)/shard_map/pallas_call | solution.py:387
  114.8 0.7 in_order.1
  115.5 4.4 %shard_map.95.refs_9_ = bf16[512,8192]{1,0:T(8,128)(2,1)} custom-call(bf16[512,1024]{1,0:T(8,128)(2,1)S(1)} %collective-permute-done.refs_0_, bf16[512,1024]{1,0:T(8,128)(2,1)S(1)} %collective-permute-done.19.refs_1_, bf16[512,1024]{1,0:T(8,128)(2,1)S(1)} %collective-permute-done.20.refs_2_, ...), custom_call_target="tpu_custom_call", output_to_operand_aliasing={{}: (7, {})} | custom-call | flops 2306867200 | bytes 7400000 | tf_op jit(solution)/shard_map/pallas_call | solution.py:387
  120.0 0.0 collective-permute-done.16.refs_3_
  120.0 6.4 %shard_map.96.refs_5_ = bf16[512,8192]{1,0:T(8,128)(2,1)} custom-call(bf16[512,1024]{1,0:T(8,128)(2,1)S(1)} %collective-permute-done.1.refs_0_, bf16[512,1024]{1,0:T(8,128)(2,1)S(1)} %collective-permute-done.4.refs_1_, bf16[512,1024]{1,0:T(8,128)(2,1)S(1)} %collective-permute-done.15.refs_2_, ...), custom_call_target="tpu_custom_call", output_to_operand_aliasing={{}: (9, {})} | custom-call | flops 3460300800 | bytes 10600000 | tf_op jit(solution)/shard_map/pallas_call | solution.py:387
  126.4 2.3 %shard_map.97.refs_5_ = bf16[512,8192]{1,0:T(8,128)(2,1)} custom-call(bf16[512,1024]{1,0:T(8,128)(2,1)S(1)} %collective-permute-done.2.refs_0_, bf16[512,1024]{1,0:T(8,128)(2,1)S(1)} %collective-permute-done.5.refs_1_, bf16[512,1024]{1,0:T(8,128)(2,1)S(1)} %copy-done, ...), custom_call_target="tpu_custom_call", output_to_operand_aliasing={{}: (5, {})} | custom-call | flops 1153433600 | bytes 4200000 | tf_op jit(solution)/shard_map/pallas_call | solution.py:387
  128.7 2.3 %shard_map.98 = bf16[512,8192]{1,0:T(8,128)(2,1)} custom-call(bf16[512,1024]{1,0:T(8,128)(2,1)S(1)} %collective-permute-done.3.refs_0_, bf16[512,1024]{1,0:T(8,128)(2,1)S(1)} %collective-permute-done.6.refs_1_, bf16[512,1024]{1,0:T(8,128)(2,1)S(1)} %copy-done, ...), custom_call_target="tpu_custom_call", output_to_operand_aliasing={{}: (5, {})} | custom-call | flops 1153433600 | bytes 4200000 | tf_op jit(solution)/shard_map/pallas_call | solution.py:387
  (20 shorter events, 0.2 us)
Async XLA Ops:
  0.6 29.1 %copy-start = (bf16[512,1024]{1,0:T(8,128)(2,1)S(1)}, bf16[512,1024]{1,0:T(8,128)(2,1)}, u32[]{:S(2)}) copy-start(bf16[512,1024]{1,0:T(8,128)(2,1)} %refs_2_.5) | copy-start | bytes 3145732
  1.6 4.8 %collective-permute-start.7 = (bf16[32,1152]{1,0:T(8,128)(2,1)S(1)}, bf16[32,1152]{1,0:T(8,128)(2,1)S(1)}, u32[]{:S(2)}, u32[]{:S(2)}) collective-permute-start(bf16[32,1152]{1,0:T(8,128)(2,1)S(1)} %pack.1.mine_ref), channel_id=1, source_target_pairs={{0,1},{1,16},{2,3},{3,18},{4,5},{5,20},{6,7},{7,22},{8,25},{9,8},{... | collective-permute-start | bytes 221192 | tf_op jit(solution)/shard_map/ppermute | solution.py:88
  6.4 6.4 %collective-permute-start.9 = (bf16[2,32,1152]{2,1,0:T(8,128)(2,1)S(1)}, bf16[2,32,1152]{2,1,0:T(8,128)(2,1)S(1)}, u32[]{:S(2)}, u32[]{:S(2)}) collective-permute-start(bf16[2,32,1152]{2,1,0:T(8,128)(2,1)S(1)} %join.1.refs_0_), channel_id=1, source_target_pairs={{0,6},{1,7},{2,0},{3,1},{4,2},{5,3},{6,4},{7,5},{8,10},{9,11},{10,... | collective-permute-start | bytes 442376 | tf_op jit(solution)/shard_map/ppermute | solution.py:88
  8.1 11.1 %collective-permute-start.8 = (bf16[2,32,1152]{2,1,0:T(8,128)(2,1)S(1)}, bf16[2,32,1152]{2,1,0:T(8,128)(2,1)S(1)}, u32[]{:S(2)}, u32[]{:S(2)}) collective-permute-start(bf16[2,32,1152]{2,1,0:T(8,128)(2,1)S(1)} %join.1.refs_0_), channel_id=1, source_target_pairs={{0,2},{1,3},{2,4},{3,5},{4,6},{5,7},{6,0},{7,1},{8,14},{9,15},{10,... | collective-permute-start | bytes 442376 | tf_op jit(solution)/shard_map/ppermute | solution.py:88
  12.8 7.5 %collective-permute-start.10 = (bf16[2,32,1152]{2,1,0:T(8,128)(2,1)S(1)}, bf16[2,32,1152]{2,1,0:T(8,128)(2,1)S(1)}, u32[]{:S(2)}, u32[]{:S(2)}) collective-permute-start(bf16[2,32,1152]{2,1,0:T(8,128)(2,1)S(1)} %collective-permute-done.9.refs_2_), channel_id=1, source_target_pairs={{0,6},{1,7},{2,0},{3,1},{4,2},{5,3},{6,4},{7,5},{8,10},{9,11},{10,... | collective-permute-start | bytes 442376 | tf_op jit(solution)/shard_map/ppermute | solution.py:88
  12.8 16.9 %collective-permute-start.11 = (bf16[2,32,1152]{2,1,0:T(8,128)(2,1)S(1)}, bf16[2,32,1152]{2,1,0:T(8,128)(2,1)S(1)}, u32[]{:S(2)}, u32[]{:S(2)}) collective-permute-start(bf16[2,32,1152]{2,1,0:T(8,128)(2,1)S(1)} %join.1.refs_0_), channel_id=1, source_target_pairs={{0,8},{1,9},{2,10},{3,11},{4,12},{5,13},{6,14},{7,15},{8,0},{9,1},... | collective-permute-start | bytes 442376 | tf_op jit(solution)/shard_map/ppermute | solution.py:88
  19.2 10.5 %collective-permute-start.12 = (bf16[2,32,1152]{2,1,0:T(8,128)(2,1)S(1)}, bf16[2,32,1152]{2,1,0:T(8,128)(2,1)S(1)}, u32[]{:S(2)}, u32[]{:S(2)}) collective-permute-start(bf16[2,32,1152]{2,1,0:T(8,128)(2,1)S(1)} %collective-permute-done.9.refs_2_), channel_id=1, source_target_pairs={{0,8},{1,9},{2,10},{3,11},{4,12},{5,13},{6,14},{7,15},{8,0},{9,1},... | collective-permute-start | bytes 442376 | tf_op jit(solution)/shard_map/ppermute | solution.py:88
  19.2 10.5 %collective-permute-start.13 = (bf16[2,32,1152]{2,1,0:T(8,128)(2,1)S(1)}, bf16[2,32,1152]{2,1,0:T(8,128)(2,1)S(1)}, u32[]{:S(2)}, u32[]{:S(2)}) collective-permute-start(bf16[2,32,1152]{2,1,0:T(8,128)(2,1)S(1)} %collective-permute-done.8.refs_1_), channel_id=1, source_target_pairs={{0,8},{1,9},{2,10},{3,11},{4,12},{5,13},{6,14},{7,15},{8,0},{9,1},... | collective-permute-start | bytes 442376 | tf_op jit(solution)/shard_map/ppermute | solution.py:88
  20.2 9.5 %collective-permute-start.14 = (bf16[2,32,1152]{2,1,0:T(8,128)(2,1)S(1)}, bf16[2,32,1152]{2,1,0:T(8,128)(2,1)S(1)}, u32[]{:S(2)}, u32[]{:S(2)}) collective-permute-start(bf16[2,32,1152]{2,1,0:T(8,128)(2,1)S(1)} %collective-permute-done.10.refs_3_), channel_id=1, source_target_pairs={{0,8},{1,9},{2,10},{3,11},{4,12},{5,13},{6,14},{7,15},{8,0},{9,1},... | collective-permute-start | bytes 442376 | tf_op jit(solution)/shard_map/ppermute | solution.py:88
  26.2 18.3 %collective-permute-start = (bf16[512,1024]{1,0:T(8,128)(2,1)S(1)}, bf16[512,1024]{1,0:T(8,128)(2,1)S(1)}, u32[]{:S(2)}, u32[]{:S(2)}) collective-permute-start(bf16[512,1024]{1,0:T(8,128)(2,1)S(1)} %get-tuple-element.17.refs_0_), channel_id=1, source_target_pairs={{0,2},{1,3},{2,4},{3,5},{4,6},{5,7},{6,0},{7,1},{8,14},{9,15},{10,... | collective-permute-start | bytes 3145736 | tf_op jit(solution)/shard_map/ppermute | solution.py:88
  34.6 2.5 %collective-permute-start.23 = (bf16[4,2,32,1152]{3,2,1,0:T(8,128)(2,1)S(1)}, bf16[4,2,32,1152]{3,2,1,0:T(8,128)(2,1)S(1)}, u32[]{:S(2)}, u32[]{:S(2)}) collective-permute-start(bf16[4,2,32,1152]{3,2,1,0:T(8,128)(2,1)S(1)} %get-tuple-element.22), channel_id=1, source_target_pairs={{0,8},{1,9},{2,10},{3,11},{4,12},{5,13},{6,14},{7,15},{8,0},{9,1},... | collective-permute-start | bytes 1769480 | tf_op jit(solution)/shard_map/ppermute | solution.py:88
  34.7 50.3 %collective-permute-start.22 = (bf16[512,1024]{1,0:T(8,128)(2,1)S(1)}, bf16[512,1024]{1,0:T(8,128)(2,1)S(1)}, u32[]{:S(2)}, u32[]{:S(2)}) collective-permute-start(bf16[512,1024]{1,0:T(8,128)(2,1)S(1)} %get-tuple-element.17.refs_0_), channel_id=1, source_target_pairs={{0,8},{1,9},{2,10},{3,11},{4,12},{5,13},{6,14},{7,15},{8,0},{9,1},... | collective-permute-start | bytes 3145736 | tf_op jit(solution)/shard_map/ppermute | solution.py:88
  35.2 50.0 %collective-permute-start.19 = (bf16[512,1024]{1,0:T(8,128)(2,1)S(1)}, bf16[512,1024]{1,0:T(8,128)(2,1)S(1)}, u32[]{:S(2)}, u32[]{:S(2)}) collective-permute-start(bf16[512,1024]{1,0:T(8,128)(2,1)S(1)} %get-tuple-element.17.refs_0_), channel_id=1, source_target_pairs={{0,1},{1,16},{2,3},{3,18},{4,5},{5,20},{6,7},{7,22},{8,25},{9,8},{... | collective-permute-start | bytes 3145736 | tf_op jit(solution)/shard_map/ppermute | solution.py:88
  37.2 7.1 %collective-permute-start.25 = (bf16[2,32,1152]{2,1,0:T(8,128)(2,1)S(1)}, bf16[2,32,1152]{2,1,0:T(8,128)(2,1)S(1)}, u32[]{:S(2)}, u32[]{:S(2)}) collective-permute-start(bf16[2,32,1152]{2,1,0:T(8,128)(2,1)S(1)} %get-tuple-element.26), channel_id=1, source_target_pairs={{0,6},{1,7},{2,0},{3,1},{4,2},{5,3},{6,4},{7,5},{8,10},{9,11},{10,... | collective-permute-start | bytes 442376 | tf_op jit(solution)/shard_map/ppermute | solution.py:88
  37.3 9.9 %collective-permute-start.24 = (bf16[2,32,1152]{2,1,0:T(8,128)(2,1)S(1)}, bf16[2,32,1152]{2,1,0:T(8,128)(2,1)S(1)}, u32[]{:S(2)}, u32[]{:S(2)}) collective-permute-start(bf16[2,32,1152]{2,1,0:T(8,128)(2,1)S(1)} %get-tuple-element.24), channel_id=1, source_target_pairs={{0,2},{1,3},{2,4},{3,5},{4,6},{5,7},{6,0},{7,1},{8,14},{9,15},{10,... | collective-permute-start | bytes 442376 | tf_op jit(solution)/shard_map/ppermute | solution.py:88
  44.4 5.7 %collective-permute-start.26 = (bf16[2,32,1152]{2,1,0:T(8,128)(2,1)S(1)}, bf16[2,32,1152]{2,1,0:T(8,128)(2,1)S(1)}, u32[]{:S(2)}, u32[]{:S(2)}) collective-permute-start(bf16[2,32,1152]{2,1,0:T(8,128)(2,1)S(1)} %shard_map.99), channel_id=1, source_target_pairs={{0,6},{1,7},{2,0},{3,1},{4,2},{5,3},{6,4},{7,5},{8,10},{9,11},{10,... | collective-permute-start | bytes 442376 | tf_op jit(solution)/shard_map/ppermute | solution.py:88
  44.5 44.5 %collective-permute-start.1 = (bf16[512,1024]{1,0:T(8,128)(2,1)S(1)}, bf16[512,1024]{1,0:T(8,128)(2,1)S(1)}, u32[]{:S(2)}, u32[]{:S(2)}) collective-permute-start(bf16[512,1024]{1,0:T(8,128)(2,1)S(1)} %collective-permute-done.refs_0_), channel_id=1, source_target_pairs={{0,2},{1,3},{2,4},{3,5},{4,6},{5,7},{6,0},{7,1},{8,14},{9,15},{10,... | collective-permute-start | bytes 3145736 | tf_op jit(solution)/shard_map/ppermute | solution.py:88
  47.2 42.8 %collective-permute-start.4 = (bf16[512,1024]{1,0:T(8,128)(2,1)S(1)}, bf16[512,1024]{1,0:T(8,128)(2,1)S(1)}, u32[]{:S(2)}, u32[]{:S(2)}) collective-permute-start(bf16[512,1024]{1,0:T(8,128)(2,1)S(1)} %collective-permute-done.refs_0_), channel_id=1, source_target_pairs={{0,1},{1,16},{2,3},{3,18},{4,5},{5,20},{6,7},{7,22},{8,25},{9,8},{... | collective-permute-start | bytes 3145736 | tf_op jit(solution)/shard_map/ppermute | solution.py:88
  50.2 5.6 %collective-permute-start.27 = (bf16[32,1152]{1,0:T(8,128)(2,1)S(1)}, bf16[32,1152]{1,0:T(8,128)(2,1)S(1)}, u32[]{:S(2)}, u32[]{:S(2)}) collective-permute-start(bf16[32,1152]{1,0:T(8,128)(2,1)S(1)} %get-tuple-element.28), channel_id=1, source_target_pairs={{0,1},{1,16},{2,3},{3,18},{4,5},{5,20},{6,7},{7,22},{8,9},{9,24},{... | collective-permute-start | bytes 221192 | tf_op jit(solution)/shard_map/ppermute | solution.py:88
  55.8 6.1 %collective-permute-start.28 = (bf16[32,1152]{1,0:T(8,128)(2,1)S(1)}, bf16[32,1152]{1,0:T(8,128)(2,1)S(1)}, u32[]{:S(2)}, u32[]{:S(2)}) collective-permute-start(bf16[32,1152]{1,0:T(8,128)(2,1)S(1)} %get-tuple-element.28), channel_id=1, source_target_pairs={{0,17},{1,0},{2,19},{3,2},{4,21},{5,4},{6,23},{7,6},{8,25},{9,8},{... | collective-permute-start | bytes 221192 | tf_op jit(solution)/shard_map/ppermute | solution.py:88
  61.9 4.7 %collective-permute-start.29 = (bf16[32,1152]{1,0:T(8,128)(2,1)S(1)}, bf16[32,1152]{1,0:T(8,128)(2,1)S(1)}, u32[]{:S(2)}, u32[]{:S(2)}) collective-permute-start(bf16[32,1152]{1,0:T(8,128)(2,1)S(1)} %get-tuple-element.27.refs_0_), channel_id=1, source_target_pairs={{0,16},{1,17},{2,18},{3,19},{4,20},{5,21},{6,22},{7,23},{8,24},{9,... | collective-permute-start | bytes 221192 | tf_op jit(solution)/shard_map/ppermute | solution.py:88
  66.6 3.3 %collective-permute-start.30 = (bf16[32,1152]{1,0:T(8,128)(2,1)S(1)}, bf16[32,1152]{1,0:T(8,128)(2,1)S(1)}, u32[]{:S(2)}, u32[]{:S(2)}) collective-permute-start(bf16[32,1152]{1,0:T(8,128)(2,1)S(1)} %shard_map.101.refs_0_), channel_id=1, source_target_pairs={{0,96},{1,97},{2,98},{3,99},{4,100},{5,101},{6,102},{7,103},{8,40}... | collective-permute-start | bytes 221192 | tf_op jit(solution)/shard_map/ppermute | solution.py:88
  69.9 4.7 %collective-permute-start.31 = (bf16[32,1152]{1,0:T(8,128)(2,1)S(1)}, bf16[32,1152]{1,0:T(8,128)(2,1)S(1)}, u32[]{:S(2)}, u32[]{:S(2)}) collective-permute-start(bf16[32,1152]{1,0:T(8,128)(2,1)S(1)} %shard_map.102.refs_0_), channel_id=1, source_target_pairs={{0,32},{1,33},{2,34},{3,35},{4,36},{5,37},{6,38},{7,39},{8,104},{9... | collective-permute-start | bytes 221192 | tf_op jit(solution)/shard_map/ppermute | solution.py:88
  74.6 11.4 %collective-permute-start.32 = (f32[32,1152]{1,0:T(8,128)S(1)}, f32[32,1152]{1,0:T(8,128)S(1)}, u32[]{:S(2)}, u32[]{:S(2)}) collective-permute-start(f32[32,1152]{1,0:T(8,128)S(1)} %shard_map.103.mine_ref), channel_id=1, source_target_pairs={{0,8},{1,9},{2,10},{3,11},{4,12},{5,13},{6,14},{7,15},{8,0},{9,1},... | collective-permute-start | bytes 442376 | tf_op jit(solution)/shard_map/ppermute | solution.py:88
  85.1 5.4 %collective-permute-start.20 = (bf16[512,1024]{1,0:T(8,128)(2,1)S(1)}, bf16[512,1024]{1,0:T(8,128)(2,1)S(1)}, u32[]{:S(2)}, u32[]{:S(2)}) collective-permute-start(bf16[512,1024]{1,0:T(8,128)(2,1)S(1)} %collective-permute-done.refs_0_), channel_id=1, source_target_pairs={{0,8},{1,9},{2,10},{3,11},{4,12},{5,13},{6,14},{7,15},{8,0},{9,1},... | collective-permute-start | bytes 3145736 | tf_op jit(solution)/shard_map/ppermute | solution.py:88
  85.2 5.3 %collective-permute-start.21 = (bf16[512,1024]{1,0:T(8,128)(2,1)S(1)}, bf16[512,1024]{1,0:T(8,128)(2,1)S(1)}, u32[]{:S(2)}, u32[]{:S(2)}) collective-permute-start(bf16[512,1024]{1,0:T(8,128)(2,1)S(1)} %collective-permute-done.19.refs_1_), channel_id=1, source_target_pairs={{0,8},{1,9},{2,10},{3,11},{4,12},{5,13},{6,14},{7,15},{8,0},{9,1},... | collective-permute-start | bytes 3145736 | tf_op jit(solution)/shard_map/ppermute | solution.py:88
  86.1 15.4 %collective-permute-start.15 = (bf16[512,1024]{1,0:T(8,128)(2,1)S(1)}, bf16[512,1024]{1,0:T(8,128)(2,1)S(1)}, u32[]{:S(2)}, u32[]{:S(2)}) collective-permute-start(bf16[512,1024]{1,0:T(8,128)(2,1)S(1)} %collective-permute-done.refs_0_), channel_id=1, source_target_pairs={{0,32},{1,33},{2,34},{3,35},{4,36},{5,37},{6,38},{7,39},{8,104},{9... | collective-permute-start | bytes 3145736 | tf_op jit(solution)/shard_map/ppermute | solution.py:88
  89.0 13.9 %collective-permute-start.2 = (bf16[512,1024]{1,0:T(8,128)(2,1)S(1)}, bf16[512,1024]{1,0:T(8,128)(2,1)S(1)}, u32[]{:S(2)}, u32[]{:S(2)}) collective-permute-start(bf16[512,1024]{1,0:T(8,128)(2,1)S(1)} %collective-permute-done.1.refs_0_), channel_id=1, source_target_pairs={{0,1},{1,16},{2,3},{3,18},{4,5},{5,20},{6,7},{7,22},{8,25},{9,8},{... | collective-permute-start | bytes 3145736 | tf_op jit(solution)/shard_map/ppermute | solution.py:88
  90.0 22.5 %collective-permute-start.5 = (bf16[512,1024]{1,0:T(8,128)(2,1)S(1)}, bf16[512,1024]{1,0:T(8,128)(2,1)S(1)}, u32[]{:S(2)}, u32[]{:S(2)}) collective-permute-start(bf16[512,1024]{1,0:T(8,128)(2,1)S(1)} %collective-permute-done.4.refs_1_), channel_id=1, source_target_pairs={{0,32},{1,33},{2,34},{3,35},{4,36},{5,37},{6,38},{7,39},{8,104},{9... | collective-permute-start | bytes 3145736 | tf_op jit(solution)/shard_map/ppermute | solution.py:88
  90.5 29.5 %collective-permute-start.16 = (bf16[512,1024]{1,0:T(8,128)(2,1)S(1)}, bf16[512,1024]{1,0:T(8,128)(2,1)S(1)}, u32[]{:S(2)}, u32[]{:S(2)}) collective-permute-start(bf16[512,1024]{1,0:T(8,128)(2,1)S(1)} %collective-permute-done.1.refs_0_), channel_id=1, source_target_pairs={{0,8},{1,9},{2,10},{3,11},{4,12},{5,13},{6,14},{7,15},{8,0},{9,1},... | collective-permute-start | bytes 3145736 | tf_op jit(solution)/shard_map/ppermute | solution.py:88
  90.5 29.5 %collective-permute-start.17 = (bf16[512,1024]{1,0:T(8,128)(2,1)S(1)}, bf16[512,1024]{1,0:T(8,128)(2,1)S(1)}, u32[]{:S(2)}, u32[]{:S(2)}) collective-permute-start(bf16[512,1024]{1,0:T(8,128)(2,1)S(1)} %collective-permute-done.4.refs_1_), channel_id=1, source_target_pairs={{0,8},{1,9},{2,10},{3,11},{4,12},{5,13},{6,14},{7,15},{8,0},{9,1},... | collective-permute-start | bytes 3145736 | tf_op jit(solution)/shard_map/ppermute | solution.py:88
  101.5 18.5 %collective-permute-start.18 = (bf16[512,1024]{1,0:T(8,128)(2,1)S(1)}, bf16[512,1024]{1,0:T(8,128)(2,1)S(1)}, u32[]{:S(2)}, u32[]{:S(2)}) collective-permute-start(bf16[512,1024]{1,0:T(8,128)(2,1)S(1)} %collective-permute-done.15.refs_2_), channel_id=1, source_target_pairs={{0,8},{1,9},{2,10},{3,11},{4,12},{5,13},{6,14},{7,15},{8,0},{9,1},... | collective-permute-start | bytes 3145736 | tf_op jit(solution)/shard_map/ppermute | solution.py:88
  103.0 25.7 %collective-permute-start.3 = (bf16[512,1024]{1,0:T(8,128)(2,1)S(1)}, bf16[512,1024]{1,0:T(8,128)(2,1)S(1)}, u32[]{:S(2)}, u32[]{:S(2)}) collective-permute-start(bf16[512,1024]{1,0:T(8,128)(2,1)S(1)} %collective-permute-done.2.refs_0_), channel_id=1, source_target_pairs={{0,8},{1,9},{2,10},{3,11},{4,12},{5,13},{6,14},{7,15},{8,0},{9,1},... | collective-permute-start | bytes 3145736 | tf_op jit(solution)/shard_map/ppermute | solution.py:88
  112.4 16.3 %collective-permute-start.6 = (bf16[512,1024]{1,0:T(8,128)(2,1)S(1)}, bf16[512,1024]{1,0:T(8,128)(2,1)S(1)}, u32[]{:S(2)}, u32[]{:S(2)}) collective-permute-start(bf16[512,1024]{1,0:T(8,128)(2,1)S(1)} %collective-permute-done.5.refs_1_), channel_id=1, source_target_pairs={{0,8},{1,9},{2,10},{3,11},{4,12},{5,13},{6,14},{7,15},{8,0},{9,1},... | collective-permute-start | bytes 3145736 | tf_op jit(solution)/shard_map/ppermute | solution.py:88
